TPU v7x, 32 devices: a whole 2x2x4 slice. The times are simulated.
32 devices in a mesh: band: 2 (over y), strip: 4 (over z), src: 4 (over x, core).
Axes of the slice: x: 2, y: 2, z: 4, core: 2. Of those that a mesh axis runs over, the one named last changes fastest.
Arguments:
- theta: float32 [1024, 512], P(('band', 'strip')), parts along dimension 0, may hold values from -8 to 8
- target: int32 [1024, 512], P(('band', 'strip')), parts along dimension 0, may hold values 0 or 1
- source_shift: int32 [32, 2], P('src'), may hold values from -16 to 16
- source_weight: float32 [32], P('src'), may hold values from 0.14 to 7.1
Outputs:
- theta_final: float32 [1024, 512], P(('band', 'strip')), parts along dimension 0
- resist: float32 [1024, 512], P(('band', 'strip')), parts along dimension 0
There are 2 independent parts, one for each index of `band`. A program takes and returns all parts, laid end to end along the dimension named above; an argument that names none is the same for every part. Nothing has to cross between parts.
All inputs are finite; a program needn't handle non-finite values. No bound on the sum of `target` on one device may be relied on, other than what follows from the above.
Results may differ from a plain program's by a relative error of at most 0.0055.
The roundings to bfloat16 on the way count: a program that leaves them out, or rounds other values in their place, can miss the bound.
Values may be sent and summed in bfloat16 or wider, within the bound.
No kernel may reach another device: no remote copies, remote signals or barrier semaphores. Data moves between devices by JAX's collectives and lax.ppermute only.
A program may use at most 64 MiB of HBM per device.

v0:
```python
import math

import jax
import jax.numpy as jnp
from jax import lax
from jax.sharding import PartitionSpec as P

ROWS = 128
COLS = 512
HALO = 64
FREQ = 128
SRC_DEV = 8
ITERS = 2


steepness = 20.0
dose_level = 0.27
step_size = 1.0
epsilon = 1e-06


def extended(cells, sides, width):
    for axis, dim in sides:
        count = lax.axis_size(axis)
        head = lax.slice_in_dim(cells, 0, width, axis=dim)
        tail = lax.slice_in_dim(cells, cells.shape[dim] - width, cells.shape[dim], axis=dim)
        cells = jnp.concatenate(
            [
                lax.ppermute(tail, axis, [(i, (i + 1) % count) for i in range(count)]),
                cells,
                lax.ppermute(head, axis, [((i + 1) % count, i) for i in range(count)]),
            ],
            axis=dim,
        )
    return cells


def shifted(array, axis, by):
    size = lax.axis_size(axis)
    return lax.ppermute(array, axis, [(i, (i + by) % size) for i in range(size)])


def phase_pair(freq_ids, points, period):
    index = freq_ids[:, None] % period * points[None, :] % period
    angle = 2.0 * math.pi / period * index.astype(jnp.float32)
    return (jnp.cos(angle), jnp.sin(angle))


def build_tables():
    freq_ids = jnp.arange(FREQ, dtype=jnp.int32) - FREQ // 2
    win_len = ROWS + 2 * HALO
    row_cos, row_sin = phase_pair(freq_ids, jnp.arange(win_len, dtype=jnp.int32), win_len)
    forward_rows = (jnp.concatenate([row_cos, -row_sin], 0) / win_len).astype(jnp.bfloat16)
    col_cos, col_sin = phase_pair(freq_ids, jnp.arange(COLS, dtype=jnp.int32), COLS)
    real_part = jnp.concatenate([col_cos.T, -col_sin.T], 1) / COLS
    imag_part = jnp.concatenate([col_sin.T, col_cos.T], 1) / COLS
    forward_cols = jnp.stack([real_part, imag_part], 0).astype(jnp.bfloat16)
    inverse_cols = jnp.concatenate(
        [jnp.concatenate([col_cos, col_sin], 1), jnp.concatenate([-col_sin, col_cos], 1)], 0
    ).astype(jnp.bfloat16)
    inner_cos, inner_sin = phase_pair(freq_ids, jnp.arange(ROWS, dtype=jnp.int32) + HALO, win_len)
    inner_cos, inner_sin = (inner_cos.T, inner_sin.T)
    inverse_rows = jnp.stack(
        [jnp.stack([inner_cos, -inner_sin], 1), jnp.stack([inner_sin, inner_cos], 1)], 0
    ).astype(jnp.bfloat16)
    return (forward_rows, forward_cols, inverse_cols, inverse_rows)


def pupil_of(shifts):
    grid = jnp.arange(FREQ, dtype=jnp.int32) - FREQ // 2
    along_k = grid[None, :] + shifts[:, 0:1]
    along_l = grid[None, :] + shifts[:, 1:2]
    radius = FREQ // 4
    inside = (
        along_k[:, :, None] * along_k[:, :, None] + along_l[:, None, :] * along_l[:, None, :]
        <= radius * radius
    )
    pupil = inside.astype(jnp.float32)
    return jnp.concatenate([pupil, pupil], 2).astype(jnp.bfloat16)


def imaging(window, pupil, weights, tables, total_sources):
    forward_rows, forward_cols, inverse_cols, inverse_rows = tables
    count = pupil.shape[0]
    half = jnp.dot(forward_rows, window, preferred_element_type=jnp.float32).astype(jnp.bfloat16)
    spectrum = jnp.einsum(
        "pkc,pcl->kl", half.reshape(2, FREQ, COLS), forward_cols, preferred_element_type=jnp.float32
    ).astype(jnp.bfloat16)
    passed = pupil * spectrum[None]
    columns = jnp.dot(
        passed.reshape(count * FREQ, 2 * FREQ), inverse_cols, preferred_element_type=jnp.float32
    ).astype(jnp.bfloat16)
    columns = columns.reshape(count, FREQ, 2, COLS)
    field = jnp.einsum("pxqk,skqc->spxc", inverse_rows, columns, preferred_element_type=jnp.float32)
    scaled = weights / total_sources
    partial_sum = jnp.sum(scaled[:, None, None, None] * field * field, axis=(0, 1))
    return (field, partial_sum)


def adjoint_spectrum(field, d_int, pupil, weights, tables, total_sources):
    forward_rows, forward_cols, inverse_cols, inverse_rows = tables
    count = pupil.shape[0]
    coeff = 2.0 * weights / total_sources
    d_field = (coeff[:, None, None, None] * d_int[None, None] * field).astype(jnp.bfloat16)
    d_columns = jnp.einsum(
        "pxqk,spxc->skqc", inverse_rows, d_field, preferred_element_type=jnp.float32
    ).astype(jnp.bfloat16)
    d_passed = jnp.dot(
        d_columns.reshape(count * FREQ, 2 * COLS),
        inverse_cols.T,
        preferred_element_type=jnp.float32,
    )
    d_passed = d_passed.reshape(count, FREQ, 2 * FREQ)
    return jnp.sum(d_passed * pupil.astype(jnp.float32), axis=0)


def adjoint_window(d_spectrum, tables):
    forward_rows, forward_cols, inverse_cols, inverse_rows = tables
    d_half = jnp.einsum(
        "kl,pcl->pkc", d_spectrum, forward_cols.astype(jnp.float32), precision=lax.Precision.HIGHEST
    )
    d_half = d_half.reshape(2 * FREQ, COLS)
    return jnp.dot(forward_rows.astype(jnp.float32).T, d_half, precision=lax.Precision.HIGHEST)


def per_device(theta, target, source_shift, source_weight):
    tables = build_tables()
    pupil = pupil_of(source_shift)
    total_sources = SRC_DEV * lax.axis_size("src")
    total_cells = ROWS * lax.axis_size("strip") * COLS
    target_rows = target.astype(jnp.float32)
    resist = jnp.zeros((ROWS, COLS), jnp.float32)
    for iteration in range(ITERS):
        mask_now = jax.nn.sigmoid(theta)
        mask_low = mask_now.astype(jnp.bfloat16)
        window = extended(mask_low, (("strip", 0),), HALO)
        field, partial_sum = imaging(window, pupil, source_weight, tables, total_sources)
        intensity = lax.psum(partial_sum, "src")
        resist = jax.nn.sigmoid(steepness * (intensity - dose_level))
        d_int = 2.0 * (resist - target_rows) * steepness * resist * (1.0 - resist)
        d_spectrum = adjoint_spectrum(field, d_int, pupil, source_weight, tables, total_sources)
        d_window = adjoint_window(lax.psum(d_spectrum, "src"), tables)
        from_next = shifted(d_window[:HALO], "strip", -1)
        from_prev = shifted(d_window[HALO + ROWS :], "strip", 1)
        gradient = d_window[HALO : HALO + ROWS]
        gradient = gradient.at[:HALO].add(from_prev)
        gradient = gradient.at[ROWS - HALO :].add(from_next)
        d_theta = gradient * mask_now * (1.0 - mask_now)
        squares = lax.psum(jnp.sum(d_theta * d_theta), "strip")
        theta = theta - step_size * d_theta * lax.rsqrt(squares / total_cells + epsilon)
    return (theta, resist)


def solution(mesh):
    return jax.shard_map(
        per_device,
        mesh=mesh,
        in_specs=(P(("band", "strip"), None), P(("band", "strip"), None), P("src", None), P("src")),
        out_specs=(P(("band", "strip"), None), P(("band", "strip"), None)),
        check_vma=False,
    )
```

profile of v0, /device:TPU:0, one launch (start us, length us, event | category | flops | bytes accessed | tf_op | source)
XLA Modules:
  0.0 241.8 jit_solution(7867009594235535132)
XLA Ops:
  7.2 1.0 fusion.78
  8.3 3.1 %collective-permute-start = (bf16[64,512]{1,0:T(8,128)(2,1)S(1)}, bf16[64,512]{1,0:T(8,128)(2,1)S(1)}, u32[]{:S(2)}, u32[]{:S(2)}) collective-permute-start(bf16[64,512]{1,0:T(8,128)(2,1)S(1)} %get-tuple-element.60), channel_id=1, source_target_pairs={{0,4},{4,8},{8,12},{12,0},{1,5},{5,9},{9,13},{13,1},{2,6},{6,10},{... | collective-permute-start | bytes 196616 | tf_op jit(solution)/shard_map/ppermute | solution.py:29
  11.4 2.1 collective-permute-start.1
  13.5 1.2 fusion.66
  14.7 1.0 negate_bitcast_fusion
  15.8 0.8 slice_bitcast_fusion.1
  16.6 0.7 broadcast_multiply_fusion.3
  17.2 0.6 fusion.77
  17.8 0.3 negate_convert_fusion.1
  18.8 0.2 fusion.16
  19.2 2.0 convolution_convert_fusion.1
  21.2 3.3 %reshape.550 = bf16[8,128,2,512]{3,2,1,0:T(2,128)(2,1)S(1)} reshape(bf16[1024,1024]{1,0:T(8,128)(2,1)} %convolution_convert_fusion.1) | data formatting | bytes 4194304 | tf_op jit(solution)/shard_map/reshape | solution.py:93
  24.5 3.0 %fusion = (f32[128,512]{0,1:T(8,128)S(1)}, f32[8,512,2,128,1]{3,1,4,2,0:T(8,128)}) fusion(f32[8]{0:T(128)S(1)} %get-tuple-element.73, bf16[1,128,2,128]{3,1,2,0:T(8,128)(2,1)S(1)} %get-tuple-element.63, bf16[1,128,2,128]{3,1,2,0:T(8,128)(2,1)S(1)} %get-tuple-element.62, bf16[8,128,2,512,1]{3,2,1,0,4:T(2,128)(2,1)S(1)} %bitcast.120), kind=kOutput, calls=%fused_computation.2 | convolution fusion | flops 540213248 | bytes 6684704 | tf_op jit(solution)/shard_map/pxqk,skqc->spxc/dot_general | solution.py:94
  27.5 0.8 copy.21
  28.6 31.8 %all-reduce.5.cloned.1.call-done = f32[128,512]{1,0:T(8,128)} async-done(((f32[128,512]{1,0:T(8,128)}), f32[128,512]{1,0:T(8,128)}) %all-reduce.5.cloned.1.call-update) | async-done | bytes 262160 | tf_op jit(solution)/shard_map/psum | solution.py:138
  60.4 1.1 subtract_multiply_fusion.3
  61.8 2.9 %bitcast_convert_fusion.1 = bf16[8,512,2,128]{3,1,2,0:T(8,128)(2,1)S(1)} fusion(f32[8,512,2,128,1]{3,1,4,2,0:T(8,128)} %get-tuple-element.83, f32[8,128,512]{1,2,0:T(8,128)S(1)} %broadcast_multiply_fusion.1, bf16[1,128,2,128]{3,1,2,0:T(8,128)(2,1)S(1)} %get-tuple-element.63, bf16[1,128,2,128]{3,1,2,0:T(8,128)(2,1)S(1)} %get-tuple-element.62), kind=kOutput, calls=%fused_computation.9 | convolution fusion | flops 540082176 | bytes 8519680 | tf_op jit(solution)/shard_map/pxqk,spxc->skqc/dot_general | solution.py:105
  64.8 1.4 fusion.14
  66.3 31.9 %all-reduce.7.cloned.1.call-done = f32[128,256]{1,0:T(8,128)} async-done(((f32[128,256]{1,0:T(8,128)}), f32[128,256]{1,0:T(8,128)}) %all-reduce.7.cloned.1.call-update) | async-done | bytes 131088 | tf_op jit(solution)/shard_map/psum | solution.py:142
  98.2 1.6 fusion.59
  99.7 0.4 fusion.91
  100.2 1.5 collective-permute-start.2
  101.8 2.4 collective-permute-start.3
  104.2 3.5 %collective-permute-done.2 = f32[64,512]{1,0:T(8,128)S(1)} collective-permute-done((f32[64,512]{1,0:T(8,128)S(1)}, f32[64,512]{1,0:T(8,128)S(1)}, u32[]{:S(2)}, u32[]{:S(2)}) %collective-permute-start.2) | collective-permute-done | bytes 131104 | tf_op jit(solution)/shard_map/ppermute | solution.py:40
  107.7 0.8 collective-permute-done.3
  108.6 0.7 multiply_reduce_fusion.1
  109.3 11.6 %psum.44 = f32[]{:T(128)} all-reduce(f32[]{:T(128)} %multiply_reduce_fusion.1), channel_id=1, replica_groups=mesh['band'=2,'strip'=4,'src'=4] {'strip'}, use_global_device_ids=true, to_apply=%region_5.6 | all-reduce | flops 1 | bytes 8 | tf_op jit(solution)/shard_map/psum | solution.py:149
  121.9 3.8 %collective-permute-start.5 = (bf16[64,512]{1,0:T(8,128)(2,1)S(1)}, bf16[64,512]{1,0:T(8,128)(2,1)S(1)}, u32[]{:S(2)}, u32[]{:S(2)}) collective-permute-start(bf16[64,512]{1,0:T(8,128)(2,1)S(1)} %get-tuple-element.59), channel_id=1, source_target_pairs={{4,0},{8,4},{12,8},{0,12},{5,1},{9,5},{13,9},{1,13},{6,2},{10,6},{... | collective-permute-start | bytes 196616 | tf_op jit(solution)/shard_map/ppermute | solution.py:31
  125.7 2.2 collective-permute-done.4
  128.2 0.2 fusion.17
  128.5 2.1 convolution_convert_fusion
  130.5 3.3 %reshape.553 = bf16[8,128,2,512]{3,2,1,0:T(2,128)(2,1)S(1)} reshape(bf16[1024,1024]{1,0:T(8,128)(2,1)} %convolution_convert_fusion) | data formatting | bytes 4194304 | tf_op jit(solution)/shard_map/reshape | solution.py:93
  133.8 3.7 %fusion.1 = (f32[128,512]{0,1:T(8,128)}, f32[8,512,2,128,1]{3,1,4,2,0:T(8,128)}) fusion(f32[8]{0:T(128)S(1)} %get-tuple-element.73, bf16[1,128,2,128]{3,1,2,0:T(8,128)(2,1)S(1)} %get-tuple-element.63, bf16[1,128,2,128]{3,1,2,0:T(8,128)(2,1)S(1)} %get-tuple-element.62, bf16[8,128,2,512,1]{3,2,1,0,4:T(2,128)(2,1)S(1)} %bitcast.121), kind=kOutput, calls=%fused_computation.3 | convolution fusion | flops 540213248 | bytes 6684704 | tf_op jit(solution)/shard_map/pxqk,skqc->spxc/dot_general | solution.py:94
  137.5 1.8 copy.26
  139.3 33.0 %all-reduce.9.cloned.1.call-done = f32[128,512]{1,0:T(8,128)} async-done(((f32[128,512]{1,0:T(8,128)}), f32[128,512]{1,0:T(8,128)}) %all-reduce.9.cloned.1.call-update) | async-done | bytes 262160 | tf_op jit(solution)/shard_map/psum | solution.py:138
  172.4 1.8 subtract_multiply_fusion.1
  174.6 3.0 %bitcast_convert_fusion = bf16[8,512,2,128]{3,1,2,0:T(8,128)(2,1)S(1)} fusion(f32[8,512,2,128,1]{3,1,4,2,0:T(8,128)} %get-tuple-element.85, f32[8,128,512]{1,2,0:T(8,128)S(1)} %broadcast_multiply_fusion, bf16[1,128,2,128]{3,1,2,0:T(8,128)(2,1)S(1)} %get-tuple-element.63, bf16[1,128,2,128]{3,1,2,0:T(8,128)(2,1)S(1)} %get-tuple-element.62), kind=kOutput, calls=%fused_computation.8 | convolution fusion | flops 540082176 | bytes 8519680 | tf_op jit(solution)/shard_map/pxqk,spxc->skqc/dot_general | solution.py:105
  177.6 1.4 fusion.15
  179.0 31.9 %all-reduce.11.cloned.1.call-done = f32[128,256]{1,0:T(8,128)} async-done(((f32[128,256]{1,0:T(8,128)}), f32[128,256]{1,0:T(8,128)}) %all-reduce.11.cloned.1.call-update) | async-done | bytes 131088 | tf_op jit(solution)/shard_map/psum | solution.py:142
  211.0 1.6 fusion.57
  212.5 0.5 fusion.92
  213.0 1.5 collective-permute-start.6
  214.6 2.4 collective-permute-start.7
  217.0 3.5 %collective-permute-done.6 = f32[64,512]{1,0:T(8,128)S(1)} collective-permute-done((f32[64,512]{1,0:T(8,128)S(1)}, f32[64,512]{1,0:T(8,128)S(1)}, u32[]{:S(2)}, u32[]{:S(2)}) %collective-permute-start.6) | collective-permute-done | bytes 131104 | tf_op jit(solution)/shard_map/ppermute | solution.py:40
  220.5 0.8 collective-permute-done.7
  221.3 0.8 multiply_reduce_fusion
  222.1 11.5 %psum.47 = f32[]{:T(128)} all-reduce(f32[]{:T(128)} %multiply_reduce_fusion), channel_id=1, replica_groups=mesh['band'=2,'strip'=4,'src'=4] {'strip'}, use_global_device_ids=true, to_apply=%region_11.12 | all-reduce | flops 1 | bytes 8 | tf_op jit(solution)/shard_map/psum | solution.py:149
  234.4 0.9 multiply_subtract_fusion
  (64 shorter events, 2.5 us)
Async XLA Ops:
  7.2 53.2 %all-reduce.5.cloned.1.call-start = ((), (), s32[]{:S(2)}) async-start(), calls=%async_computation | async-start | bytes 524288 | tf_op jit(solution)/shard_map/psum | solution.py:138
  8.3 10.3 %collective-permute-start = (bf16[64,512]{1,0:T(8,128)(2,1)S(1)}, bf16[64,512]{1,0:T(8,128)(2,1)S(1)}, u32[]{:S(2)}, u32[]{:S(2)}) collective-permute-start(bf16[64,512]{1,0:T(8,128)(2,1)S(1)} %get-tuple-element.60), channel_id=1, source_target_pairs={{0,4},{4,8},{8,12},{12,0},{1,5},{5,9},{9,13},{13,1},{2,6},{6,10},{... | collective-permute-start | bytes 196616 | tf_op jit(solution)/shard_map/ppermute | solution.py:29
  11.4 7.2 %collective-permute-start.1 = (bf16[64,512]{1,0:T(8,128)(2,1)S(1)}, bf16[64,512]{1,0:T(8,128)(2,1)S(1)}, u32[]{:S(2)}, u32[]{:S(2)}) collective-permute-start(bf16[64,512]{1,0:T(8,128)(2,1)S(1)} %get-tuple-element.61), channel_id=1, source_target_pairs={{4,0},{8,4},{12,8},{0,12},{5,1},{9,5},{13,9},{1,13},{6,2},{10,6},{... | collective-permute-start | bytes 196616 | tf_op jit(solution)/shard_map/ppermute | solution.py:31
  14.7 4.4 %copy-start.2 = (bf16[128,512]{1,0:T(8,128)(2,1)}, bf16[128,512]{1,0:T(8,128)(2,1)S(1)}, u32[]{:S(2)}) copy-start(bf16[128,512]{1,0:T(8,128)(2,1)S(1)} %get-tuple-element.75) | copy-start | bytes 393220
  14.7 4.4 %copy-start.5 = (bf16[128,512]{1,0:T(8,128)(2,1)}, bf16[128,512]{1,0:T(8,128)(2,1)S(1)}, u32[]{:S(2)}) copy-start(bf16[128,512]{1,0:T(8,128)(2,1)S(1)} %get-tuple-element.76) | copy-start | bytes 393220
  18.5 0.7 copy-start.8
  24.5 35.9 %copy-start.1 = (s32[128,512]{1,0:T(8,128)S(1)}, s32[128,512]{1,0:T(8,128)}, u32[]{:S(2)}) copy-start(s32[128,512]{1,0:T(8,128)} %param.13) | copy-start | bytes 786436
  28.4 69.8 %all-reduce.7.cloned.1.call-start = ((), (), s32[]{:S(2)}) async-start(), calls=%async_computation.1 | async-start | bytes 262144 | tf_op jit(solution)/shard_map/psum | solution.py:142
  28.6 36.2 %copy-start.10 = (pred[8,128,128]{2,1,0:T(32,128)(4,1)}, pred[8,128,128]{2,1,0:T(32,128)(4,1)S(1)}, u32[]{:S(2)}) copy-start(pred[8,128,128]{2,1,0:T(32,128)(4,1)S(1)} %add_compare_fusion) | copy-start | bytes 393220
  61.8 3.0 %copy-start.3 = (bf16[128,512]{1,0:T(8,128)(2,1)S(1)}, bf16[128,512]{1,0:T(8,128)(2,1)}, u32[]{:S(2)}) copy-start(bf16[128,512]{1,0:T(8,128)(2,1)} %copy-done.2) | copy-start | bytes 393220
  61.8 3.0 %copy-start.6 = (bf16[128,512]{1,0:T(8,128)(2,1)S(1)}, bf16[128,512]{1,0:T(8,128)(2,1)}, u32[]{:S(2)}) copy-start(bf16[128,512]{1,0:T(8,128)(2,1)} %copy-done.5) | copy-start | bytes 393220
  66.3 42.3 %copy-start = (f32[128,512]{1,0:T(8,128)S(1)}, f32[128,512]{1,0:T(8,128)}, u32[]{:S(2)}) copy-start(f32[128,512]{1,0:T(8,128)} %param.12) | copy-start | bytes 786436
  66.3 106.1 %all-reduce.9.cloned.1.call-start = ((), (), s32[]{:S(2)}) async-start(), calls=%async_computation.2 | async-start | bytes 524288 | tf_op jit(solution)/shard_map/psum | solution.py:138
  100.2 7.4 %collective-permute-start.2 = (f32[64,512]{1,0:T(8,128)S(1)}, f32[64,512]{1,0:T(8,128)S(1)}, u32[]{:S(2)}, u32[]{:S(2)}) collective-permute-start(f32[64,512]{1,0:T(8,128)S(1)} %get-tuple-element.55), channel_id=1, source_target_pairs={{0,4},{4,8},{8,12},{12,0},{1,5},{5,9},{9,13},{13,1},{2,6},{6,10},{... | collective-permute-start | bytes 393224 | tf_op jit(solution)/shard_map/ppermute | solution.py:40
  101.8 6.8 %collective-permute-start.3 = (f32[64,512]{1,0:T(8,128)S(1)}, f32[64,512]{1,0:T(8,128)S(1)}, u32[]{:S(2)}, u32[]{:S(2)}) collective-permute-start(f32[64,512]{1,0:T(8,128)S(1)} %get-tuple-element.54), channel_id=1, source_target_pairs={{0,12},{4,0},{8,4},{12,8},{1,13},{5,1},{9,5},{13,9},{2,14},{6,2},{... | collective-permute-start | bytes 393224 | tf_op jit(solution)/shard_map/ppermute | solution.py:40
  108.6 19.9 %copy-start.9 = (pred[1024,128]{1,0:T(32,128)(4,1)S(1)}, pred[1024,128]{1,0:T(32,128)(4,1)}, u32[]{:S(2)}) copy-start(pred[1024,128]{1,0:T(32,128)(4,1)} %copy-done.8) | copy-start | bytes 393220
  121.8 6.1 %collective-permute-start.4 = (bf16[64,512]{1,0:T(8,128)(2,1)S(1)}, bf16[64,512]{1,0:T(8,128)(2,1)S(1)}, u32[]{:S(2)}, u32[]{:S(2)}) collective-permute-start(bf16[64,512]{1,0:T(8,128)(2,1)S(1)} %get-tuple-element.58), channel_id=1, source_target_pairs={{0,4},{4,8},{8,12},{12,0},{1,5},{5,9},{9,13},{13,1},{2,6},{6,10},{... | collective-permute-start | bytes 196616 | tf_op jit(solution)/shard_map/ppermute | solution.py:29
  121.9 6.1 %collective-permute-start.5 = (bf16[64,512]{1,0:T(8,128)(2,1)S(1)}, bf16[64,512]{1,0:T(8,128)(2,1)S(1)}, u32[]{:S(2)}, u32[]{:S(2)}) collective-permute-start(bf16[64,512]{1,0:T(8,128)(2,1)S(1)} %get-tuple-element.59), channel_id=1, source_target_pairs={{4,0},{8,4},{12,8},{0,12},{5,1},{9,5},{13,9},{1,13},{6,2},{10,6},{... | collective-permute-start | bytes 196616 | tf_op jit(solution)/shard_map/ppermute | solution.py:31
  139.3 71.7 %all-reduce.11.cloned.1.call-start = ((), (), s32[]{:S(2)}) async-start(), calls=%async_computation.3 | async-start | bytes 262144 | tf_op jit(solution)/shard_map/psum | solution.py:142
  174.6 3.0 %copy-start.4 = (bf16[128,512]{1,0:T(8,128)(2,1)S(1)}, bf16[128,512]{1,0:T(8,128)(2,1)}, u32[]{:S(2)}) copy-start(bf16[128,512]{1,0:T(8,128)(2,1)} %copy-done.2) | copy-start | bytes 393220
  174.6 3.0 %copy-start.7 = (bf16[128,512]{1,0:T(8,128)(2,1)S(1)}, bf16[128,512]{1,0:T(8,128)(2,1)}, u32[]{:S(2)}) copy-start(bf16[128,512]{1,0:T(8,128)(2,1)} %copy-done.5) | copy-start | bytes 393220
  174.6 3.0 %copy-start.11 = (pred[8,128,128]{2,1,0:T(32,128)(4,1)S(1)}, pred[8,128,128]{2,1,0:T(32,128)(4,1)}, u32[]{:S(2)}) copy-start(pred[8,128,128]{2,1,0:T(32,128)(4,1)} %copy-done.10) | copy-start | bytes 393220
  213.0 7.4 %collective-permute-start.6 = (f32[64,512]{1,0:T(8,128)S(1)}, f32[64,512]{1,0:T(8,128)S(1)}, u32[]{:S(2)}, u32[]{:S(2)}) collective-permute-start(f32[64,512]{1,0:T(8,128)S(1)} %get-tuple-element.53), channel_id=1, source_target_pairs={{0,4},{4,8},{8,12},{12,0},{1,5},{5,9},{9,13},{13,1},{2,6},{6,10},{... | collective-permute-start | bytes 393224 | tf_op jit(solution)/shard_map/ppermute | solution.py:40
  214.6 6.7 %collective-permute-start.7 = (f32[64,512]{1,0:T(8,128)S(1)}, f32[64,512]{1,0:T(8,128)S(1)}, u32[]{:S(2)}, u32[]{:S(2)}) collective-permute-start(f32[64,512]{1,0:T(8,128)S(1)} %get-tuple-element.52), channel_id=1, source_target_pairs={{0,12},{4,0},{8,4},{12,8},{1,13},{5,1},{9,5},{13,9},{2,14},{6,2},{... | collective-permute-start | bytes 393224 | tf_op jit(solution)/shard_map/ppermute | solution.py:40
Sparse Core Ops, SparseCore 0:
  28.5 31.8 all-reduce.4
  66.4 31.7 all-reduce.6
  139.4 32.9 all-reduce.8
  179.2 31.7 all-reduce.10
where the time goes:
time: 242 us
  waiting for transfers between devices  140 us (58%)
  matrix products  24.4 us (10%)
  blocking collectives  23.1 us (10%)
  starting transfers between devices  17.1 us (7%)
  between operations  15.6 us (6%)
  other arithmetic  11.5 us (5%)
  local copies, waits for them, and re-layouts  10.5 us (4%)
    psum x2, waiting for transfers between devices, per_device(): intensity = lax.psum(partial_sum, 'src')  64.8 us
    psum x2, waiting for transfers between devices, per_device(): d_window = adjoint_window(lax.psum(d_spectrum, 'src'), tables)  63.8 us
    psum x2, blocking collectives, per_device(): squares = lax.psum(jnp.sum(d_theta * d_theta), 'strip')  23.1 us
    ppermute x4, waiting for transfers between devices, shifted(): lax.ppermute(array, axis, [(i, (i + by) % size) for i in range(size)])  8.66 us
    ppermute x4, starting transfers between devices, shifted(): lax.ppermute(array, axis, [(i, (i + by) % size) for i in range(size)])  7.86 us
    dot_general x2, matrix products, imaging(): jnp.einsum('pxqk,skqc->spxc', inverse_rows, columns, preferred_element_ty...  6.63 us
    reshape x2, local copies, waits for them, and re-layouts, imaging(): columns = columns.reshape(count, FREQ, 2, COLS)  6.61 us
    ppermute x2, starting transfers between devices, extended(): lax.ppermute(head, axis, [((i + 1) % count, i) for i in range(count)])  5.9 us
  transfers between devices with their start and end apart: 12, of which 9 were waited for; matrix products, arithmetic and copies ran while one was open for 2% of the time, Pallas kernels for 0%

commit v1 on v0

v1 whole, which is shorter than its diff:
```python
import functools
import math

import jax
import jax.numpy as jnp
import numpy as np
from jax import lax
from jax.experimental import pallas as pl
from jax.experimental.pallas import tpu as pltpu
from jax.sharding import PartitionSpec as P

HALO = 64
FREQ = 128
ITERS = 2

steepness = 20.0
dose_level = 0.27
step_size = 1.0
epsilon = 1e-06

RADIUS = FREQ // 4
MAX_SHIFT = FREQ // 8
LOW = FREQ // 2 - RADIUS - MAX_SHIFT
KEEP = FREQ - LOW
ALIGN = 16
SPAN = 2 * RADIUS + ALIGN
VARIANTS = 2 * MAX_SHIFT // ALIGN + 1
SPLIT = 2
GROUP = 8


def shifted(array, axis, by):
    size = lax.axis_size(axis)
    return lax.ppermute(array, axis, [(i, (i + by) % size) for i in range(size)])


def partner(array):
    size = lax.axis_size("src")
    return lax.ppermute(array, "src", [(i, i ^ 1) for i in range(size)])


def phase_pair(freq_ids, points, period):
    index = freq_ids[:, None] % period * points[None, :] % period
    angle = np.float32(2.0 * math.pi / period) * index.astype(np.float32)
    return (np.cos(angle), np.sin(angle))


@functools.lru_cache(maxsize=None)
def build_tables(rows, cols):
    low = jnp.bfloat16
    freq_ids = np.arange(FREQ, dtype=np.int32) - FREQ // 2
    win_len = rows + 2 * HALO
    row_cos, row_sin = phase_pair(freq_ids, np.arange(win_len, dtype=np.int32), win_len)
    forward_rows = (np.concatenate([row_cos, -row_sin], 0) / np.float32(win_len)).astype(low)
    col_cos, col_sin = phase_pair(freq_ids, np.arange(cols, dtype=np.int32), cols)
    real_part = np.concatenate([col_cos.T, -col_sin.T], 1) / np.float32(cols)
    imag_part = np.concatenate([col_sin.T, col_cos.T], 1) / np.float32(cols)
    forward_cols = np.stack([real_part, imag_part], 0).astype(low)
    halves = []
    for part in range(SPLIT):
        at = slice(part * cols // SPLIT, (part + 1) * cols // SPLIT)
        halves.append(
            np.concatenate(
                [
                    np.concatenate([col_cos[:, at], col_sin[:, at]], 1),
                    np.concatenate([-col_sin[:, at], col_cos[:, at]], 1),
                ],
                0,
            )
        )
    inverse_cols = np.stack(halves, 0).astype(low)
    inner_cos, inner_sin = phase_pair(freq_ids, np.arange(rows, dtype=np.int32) + HALO, win_len)
    inner_cos, inner_sin = (inner_cos.T, inner_sin.T)
    inverse_rows = np.stack(
        [np.stack([inner_cos, -inner_sin], 1), np.stack([inner_sin, inner_cos], 1)], 0
    ).astype(low)
    windows = np.stack(
        [
            inverse_rows[:, :, :, LOW + v * ALIGN : LOW + v * ALIGN + SPAN].reshape(2 * rows, 2 * SPAN)
            for v in range(VARIANTS)
        ],
        0,
    )
    inverse_rows_t = inverse_rows.transpose(2, 3, 0, 1).reshape(2 * FREQ, 2 * rows)
    return (forward_rows, np.ascontiguousarray(forward_rows.T), forward_cols, inverse_cols, windows, np.ascontiguousarray(inverse_rows_t))


def dot(a, b):
    return jnp.dot(a, b, preferred_element_type=jnp.float32)


def dot_t(a, b):
    return lax.dot_general(a, b, (((1,), (1,)), ((), ())), preferred_element_type=jnp.float32)


def window_of(shift_ref, s):
    base = RADIUS + (FREQ // 2 - 2 * RADIUS) - shift_ref[s, 0]
    return pl.multiple_of(lax.shift_left(lax.shift_right_logical(base, 4), 4), ALIGN)


def image(mask, shift_ref, weight_ref, tables, target_ref, partial_ref, resist_ref, scratch, rows):
    fr_ref, fc_ref, gc_ref, grw_ref, grt_ref = tables
    spec_ref, pupil_ref, cols_ref, field_ref, dcols_ref, inten_ref, acc_ref = scratch
    sources = field_ref.shape[0]
    width = field_ref.shape[2]
    half = dot(fr_ref[...], mask).astype(jnp.bfloat16)
    spectrum = dot(half[:FREQ], fc_ref[0]) + dot(half[FREQ:], fc_ref[1])
    spec_ref[...] = spectrum.astype(jnp.bfloat16).astype(jnp.float32)
    inten_ref[...] = jnp.zeros_like(inten_ref)
    acc_ref[...] = jnp.zeros_like(acc_ref)

    def to_columns(g, carry):
        pieces = []
        for i in range(GROUP):
            s = g * GROUP + i
            base = window_of(shift_ref, s)
            along_k = lax.broadcasted_iota(jnp.int32, (SPAN, FREQ), 0) + (base - FREQ // 2 + shift_ref[s, 0])
            along_l = lax.broadcasted_iota(jnp.int32, (SPAN, FREQ), 1) + (shift_ref[s, 1] - FREQ // 2)
            inside = along_k * along_k + along_l * along_l <= RADIUS * RADIUS
            pupil = jnp.where(inside, 1.0, 0.0)
            pupil_ref[s] = pupil
            part = spec_ref[pl.ds(base, SPAN), :]
            pieces.append((part * jnp.concatenate([pupil, pupil], 1)).astype(jnp.bfloat16))
        out = dot(jnp.concatenate(pieces, 0), gc_ref[0]).astype(jnp.bfloat16)
        for i in range(GROUP):
            s = g * GROUP + i
            cols_ref[s, :SPAN, :] = out[i * SPAN : (i + 1) * SPAN, :width]
            cols_ref[s, SPAN:, :] = out[i * SPAN : (i + 1) * SPAN, width:]
        return carry

    lax.fori_loop(0, sources // GROUP, to_columns, 0)

    step = 4

    def to_field(g, carry):
        total = inten_ref[...]
        for i in range(step):
            s = g * step + i
            variant = lax.shift_right_logical(window_of(shift_ref, s) - LOW, 4)
            field = dot(grw_ref[variant], cols_ref[s])
            field_ref[s] = field
            scaled = weight_ref[s] * (1.0 / sources)
            total = total + scaled * (field[:rows] * field[:rows] + field[rows:] * field[rows:])
        inten_ref[...] = total
        return carry

    lax.fori_loop(0, sources // step, to_field, 0)

    resist = jax.nn.sigmoid(steepness * (inten_ref[...] - dose_level))
    if resist_ref is not None:
        resist_ref[...] = resist
    goal = target_ref[...].astype(jnp.float32)
    inten_ref[...] = 2.0 * (resist - goal) * steepness * resist * (1.0 - resist)

    def to_d_columns(g, carry):
        d_int = inten_ref[...]
        for i in range(step):
            s = g * step + i
            base = window_of(shift_ref, s)
            scale = d_int * (2.0 * weight_ref[s] * (1.0 / sources))
            d_field = (field_ref[s] * jnp.concatenate([scale, scale], 0)).astype(jnp.bfloat16)
            table = jnp.concatenate([grt_ref[pl.ds(base, SPAN), :], grt_ref[pl.ds(base + FREQ, SPAN), :]], 0)
            d_cols = dot(table, d_field).astype(jnp.bfloat16)
            dcols_ref[s, :, :width] = d_cols[:SPAN]
            dcols_ref[s, :, width:] = d_cols[SPAN:]
        return carry

    lax.fori_loop(0, sources // step, to_d_columns, 0)

    def to_d_spectrum(g, carry):
        d_cols = dcols_ref[pl.ds(g * GROUP, GROUP)].reshape(GROUP * SPAN, 2 * width)
        d_passed = dot_t(d_cols, gc_ref[0])
        for i in range(GROUP):
            s = g * GROUP + i
            base = window_of(shift_ref, s)
            pupil = pupil_ref[s]
            part = d_passed[i * SPAN : (i + 1) * SPAN] * jnp.concatenate([pupil, pupil], 1)
            acc_ref[pl.ds(base, SPAN), :] = acc_ref[pl.ds(base, SPAN), :] + part
        return carry

    lax.fori_loop(0, sources // GROUP, to_d_spectrum, 0)
    partial_ref[...] = acc_ref[LOW:, :].astype(partial_ref.dtype)


def d_windows(mine, other, fc_ref, frt_ref, dhi_ref, dlo_ref, field_ref):
    count = len(mine)
    width = field_ref.shape[2]
    zero = jnp.zeros((LOW, 2 * FREQ), jnp.bfloat16)
    for o in range(count):
        total = mine[o][...].astype(jnp.float32) + other[o][...].astype(jnp.float32)
        high = total.astype(jnp.bfloat16)
        rest = (total - high.astype(jnp.float32)).astype(jnp.bfloat16)
        high = jnp.concatenate([zero, high], 0)
        rest = jnp.concatenate([zero, rest], 0)
        for p in range(2):
            d_half = dot_t(high, fc_ref[p]) + dot_t(rest, fc_ref[p])
            d_high = d_half.astype(jnp.bfloat16)
            dhi_ref[o, p * FREQ : (p + 1) * FREQ, :] = d_high
            dlo_ref[o, p * FREQ : (p + 1) * FREQ, :] = (d_half - d_high.astype(jnp.float32)).astype(jnp.bfloat16)
    for o in range(count):
        d_win = dot(frt_ref[...], dhi_ref[o]) + dot(frt_ref[...], dlo_ref[o])
        for h in range(SPLIT):
            field_ref[SPLIT * o + h] = d_win[:, h * width : (h + 1) * width]


def d_block(field_ref, i, count, rows):
    prev = (i - 1) % count
    return jnp.concatenate(
        [field_ref[SPLIT * i + h, :rows, :] + field_ref[SPLIT * prev + h, rows:, :] for h in range(SPLIT)], 1
    )


def put_block(field_ref, i, rows, value):
    width = field_ref.shape[2]
    for h in range(SPLIT):
        field_ref[SPLIT * i + h, :rows, :] = value[:, h * width : (h + 1) * width]


def get_block(field_ref, i, rows):
    return jnp.concatenate([field_ref[SPLIT * i + h, :rows, :] for h in range(SPLIT)], 1)


def gradients(blocks, field_ref, rows, cols):
    count = len(blocks)
    squares = jnp.zeros((1, 1), jnp.float32)
    for i, block in enumerate(blocks):
        m = jax.nn.sigmoid(block())
        d_theta = d_block(field_ref, i, count, rows) * m * (1.0 - m)
        put_block(field_ref, i, rows, d_theta)
        squares = squares + jnp.sum(d_theta * d_theta, axis=(0, 1), keepdims=True)
    return step_size * lax.rsqrt(squares / (rows * count * cols) + epsilon)


def blocks_of(prev_ref, own_ref, next_ref, rest_refs, rows):
    pieces = [(prev_ref, 0), (own_ref, 0), (own_ref, HALO), (next_ref, 0)]
    for ref in rest_refs:
        pieces += [(ref, at) for at in range(0, ref.shape[0], HALO)]
    per = rows // HALO

    def load(i):
        return jnp.concatenate(
            [ref[at : at + HALO, :].astype(jnp.float32) for ref, at in pieces[i * per : (i + 1) * per]], 0
        )

    return [functools.partial(load, i) for i in range(len(pieces) // per)]


def first_kernel(half_ref, shift_ref, weight_ref, prev_ref, own_ref, next_ref, target_ref, fr_ref, frt_ref, fc_ref, gc_ref, grw_ref, grt_ref, partial_ref, *scratch):
    rows = own_ref.shape[0]
    theta = jnp.concatenate([prev_ref[...], own_ref[...], next_ref[...]], 0)
    mask = jax.nn.sigmoid(theta).astype(jnp.bfloat16)
    image(mask, shift_ref, weight_ref, (fr_ref, fc_ref, gc_ref, grw_ref, grt_ref), target_ref, partial_ref, None, scratch, rows)


def later_kernel(count, rests, *refs):
    half_ref, shift_ref, weight_ref = refs[:3]
    refs = refs[3:]
    mine, other, refs = refs[:count], refs[count : 2 * count], refs[2 * count :]
    prev_ref, own_ref, next_ref = refs[:3]
    rest_refs, refs = refs[3 : 3 + rests], refs[3 + rests :]
    target_ref, fr_ref, frt_ref, fc_ref, gc_ref, grw_ref, grt_ref = refs[:7]
    partial_ref, resist_ref, prev_out, own_out, next_out, rest_out = refs[7:13]
    scratch, (dhi_ref, dlo_ref) = refs[13:20], refs[20:]
    field_ref = scratch[3]
    rows, cols = own_ref.shape
    d_windows(mine, other, fc_ref, frt_ref, dhi_ref, dlo_ref, field_ref)
    blocks = blocks_of(prev_ref, own_ref, next_ref, rest_refs, rows)
    factor = gradients(blocks, field_ref, rows, cols)
    masks = []
    for i, block in enumerate(blocks):
        theta = block() - get_block(field_ref, i, rows) * factor
        if i == 0:
            prev_out[...] = theta[:HALO]
            own_out[:HALO, :] = theta[HALO:]
        elif i == 1:
            own_out[HALO:, :] = theta[: rows - HALO]
            next_out[...] = theta[rows - HALO :]
        else:
            rest_out[(i - 2) * rows : (i - 1) * rows, :] = theta
        if i < 2:
            masks.append(jax.nn.sigmoid(theta).astype(jnp.bfloat16))
    image(jnp.concatenate(masks, 0), shift_ref, weight_ref, (fr_ref, fc_ref, gc_ref, grw_ref, grt_ref), target_ref, partial_ref, resist_ref, scratch, rows)


def last_kernel(count, rests, *refs):
    half_ref = refs[0]
    refs = refs[1:]
    mine, other, refs = refs[:count], refs[count : 2 * count], refs[2 * count :]
    prev_ref, own_ref, next_ref = refs[:3]
    rest_refs, refs = refs[3 : 3 + rests], refs[3 + rests :]
    fc_ref, frt_ref, resist_ref, resist_other, theta_out, resist_out, field_ref, dhi_ref, dlo_ref = refs
    rows, cols = own_ref.shape
    width = resist_ref.shape[1]
    d_windows(mine, other, fc_ref, frt_ref, dhi_ref, dlo_ref, field_ref)
    blocks = blocks_of(prev_ref, own_ref, next_ref, rest_refs, rows)
    factor = gradients(blocks, field_ref, rows, cols)
    d_own = jnp.concatenate([get_block(field_ref, 0, rows)[HALO:], get_block(field_ref, 1, rows)[: rows - HALO]], 0)
    theta_out[...] = own_ref[...] - d_own * factor
    first = half_ref[0] == 0
    resist_out[:, :width] = jnp.where(first, resist_ref[...], resist_other[...])
    resist_out[:, width:] = jnp.where(first, resist_other[...], resist_ref[...])


def per_device(theta, target, source_shift, source_weight):
    rows, cols = theta.shape
    count = lax.axis_size("strip")
    width = cols // SPLIT
    sources = source_weight.shape[0] * lax.axis_size("src")
    half = (lax.axis_index("src") % SPLIT).astype(jnp.int32).reshape(1)
    forward_rows, forward_rows_t, forward_cols, inverse_cols, windows, inverse_rows_t = [
        jnp.asarray(t) for t in build_tables(rows, cols)
    ]

    packed = jnp.concatenate([source_shift.astype(jnp.float32), source_weight[:, None]], 1)
    prev_rows = shifted(theta[rows - HALO :], "strip", 1)
    next_rows = shifted(theta[:HALO], "strip", -1)
    packed = lax.all_gather(packed, "src", axis=0, tiled=True)
    shifts = packed[:, :2].astype(jnp.int32)
    weights = packed[:, 2]

    low = theta.astype(jnp.bfloat16)
    rest = [shifted(low[rows - HALO :], "strip", -1)]
    rest += [shifted(low, "strip", -o) for o in range(2, count - 1)]
    rest += [shifted(low[:HALO], "strip", 1)]

    vmem = pl.BlockSpec(memory_space=pltpu.VMEM)
    smem = pl.BlockSpec(memory_space=pltpu.SMEM)

    def full(shape):
        return pl.BlockSpec(shape, lambda i, at: (0,) * len(shape))

    def column_half(shape):
        return pl.BlockSpec(shape, lambda i, at: (0, at[0]))

    cut = pl.BlockSpec((1, 2 * FREQ, SPLIT * width), lambda i, at: (at[0], 0, 0))
    table_specs = [
        full(forward_rows.shape), full(forward_rows_t.shape), full(forward_cols.shape), cut,
        full(windows.shape), full(inverse_rows_t.shape),
    ]
    tables = (forward_rows, forward_rows_t, forward_cols, inverse_cols, windows, inverse_rows_t)
    image_scratch = [
        pltpu.VMEM((FREQ, 2 * FREQ), jnp.float32),
        pltpu.VMEM((sources, SPAN, FREQ), jnp.float32),
        pltpu.VMEM((sources, 2 * SPAN, width), jnp.bfloat16),
        pltpu.VMEM((sources, 2 * rows, width), jnp.float32),
        pltpu.VMEM((sources, SPAN, 2 * width), jnp.bfloat16),
        pltpu.VMEM((rows, width), jnp.float32),
        pltpu.VMEM((FREQ, 2 * FREQ), jnp.float32),
    ]
    adjoint_scratch = [pltpu.VMEM((count, 2 * FREQ, cols), jnp.bfloat16)] * 2
    params = pltpu.CompilerParams(vmem_limit_bytes=60 << 20)
    cost = pl.CostEstimate(flops=6 << 30, bytes_accessed=4 << 20, transcendentals=1 << 20)
    small_cost = pl.CostEstimate(flops=1 << 30, bytes_accessed=4 << 20, transcendentals=1 << 20)

    def call(kernel, in_specs, out_shapes, out_specs, scratch, args, estimate, name):
        return pl.pallas_call(
            kernel,
            out_shape=out_shapes,
            grid_spec=pltpu.PrefetchScalarGridSpec(
                num_scalar_prefetch=1, grid=(1,), in_specs=in_specs, out_specs=out_specs, scratch_shapes=scratch
            ),
            compiler_params=params,
            cost_estimate=estimate,
            name=name,
        )(half, *args)

    f32 = jnp.float32
    partial_shape = jax.ShapeDtypeStruct((KEEP, 2 * FREQ), f32)
    final_shape = jax.ShapeDtypeStruct((KEEP, 2 * FREQ), jnp.bfloat16)
    state = [prev_rows, theta, next_rows]
    (partial,) = call(
        first_kernel,
        [smem, smem] + [full(a.shape) for a in state] + [column_half((rows, width))] + table_specs,
        [partial_shape],
        [full(partial_shape.shape)],
        image_scratch,
        [shifts, weights, *state, target, *tables],
        cost,
        "first_image",
    )
    for later in range(1, ITERS):
        mine = [partial] + [shifted(partial, "strip", -o) for o in range(1, count)]
        other = [partner(a) for a in mine]
        args = [*mine, *other, *state, *rest]
        outs = [
            final_shape if later == ITERS - 1 else partial_shape,
            jax.ShapeDtypeStruct((rows, width), f32),
            *[jax.ShapeDtypeStruct(a.shape, f32) for a in state],
            jax.ShapeDtypeStruct(((count - 2) * rows, cols), f32),
        ]
        partial, resist, *moved = call(
            functools.partial(later_kernel, count, len(rest)),
            [smem, smem] + [full(a.shape) for a in args] + [column_half((rows, width))] + table_specs,
            outs,
            [full(a.shape) for a in outs],
            image_scratch + adjoint_scratch,
            [shifts, weights, *args, target, *tables],
            cost,
            "later_image",
        )
        state, rest = moved[:3], moved[3:]
    mine = [partial] + [shifted(partial, "strip", -o) for o in range(1, count)]
    other = [partner(a) for a in mine]
    resist_other = partner(resist)
    args = [*mine, *other, *state, *rest, forward_cols, forward_rows_t, resist, resist_other]
    outs = [jax.ShapeDtypeStruct((rows, cols), f32)] * 2
    theta, resist = call(
        functools.partial(last_kernel, count, len(rest)),
        [full(a.shape) for a in args],
        outs,
        [full(a.shape) for a in outs],
        [pltpu.VMEM((SPLIT * count, 2 * rows, width), f32)] + adjoint_scratch,
        args,
        small_cost,
        "last_step",
    )
    return (theta, resist)


def solution(mesh):
    return jax.shard_map(
        per_device,
        mesh=mesh,
        in_specs=(P(("band", "strip"), None), P(("band", "strip"), None), P("src", None), P("src")),
        out_specs=(P(("band", "strip"), None), P(("band", "strip"), None)),
        check_vma=False,
    )
```

time: 242 us -> 79.2 us (0.33)
  waiting for transfers between devices: 140 us -> 16.4 us
  Pallas kernels: 0 us -> 28.2 us
  matrix products: 24.4 us -> 0 us
  blocking collectives: 23.1 us -> 5.18 us
  between operations: 15.6 us -> 0.87 us
  other arithmetic: 11.5 us -> 0.64 us
  starting transfers between devices: 17.1 us -> 21.9 us
  local copies, waits for them, and re-layouts: 10.5 us -> 5.84 us
    psum x4 -> x0, waiting for transfers between devices: 129 us -> none  [the longest x2 64.8 us: per_device(): intensity = lax.psum(partial_sum, 'src')]
    pallas_call x0 -> x3, Pallas kernels: none -> 28.2 us  [call(): pl.pallas_call(kernel, out_shape=out_shapes, grid_spec=pltpu.PrefetchScal...]
    dot_general x16 -> x0, matrix products: 24.4 us -> none  [the longest x2 6.63 us: imaging(): jnp.einsum('pxqk,skqc->spxc', inverse_rows, columns, preferred_element_ty...]
    psum x2 -> x0, blocking collectives: 23.1 us -> none  [per_device(): squares = lax.psum(jnp.sum(d_theta * d_theta), 'strip')]
    ppermute x4 -> x11, starting transfers between devices: 7.86 us -> 20.2 us  [shifted(): lax.ppermute(array, axis, [(i, (i + by) % size) for i in range(size)])]
    ppermute x4 -> x9, starting transfers between devices: 9.07 us -> 1.69 us  [partner(): return lax.ppermute(array, 'src', [(i, i ^ 1) for i in range(size)])]
    ppermute x4 -> x11, waiting for transfers between devices: 8.66 us -> 15.5 us  [shifted(): lax.ppermute(array, axis, [(i, (i + by) % size) for i in range(size)])]
    reshape x2 -> x0, local copies, waits for them, and re-layouts: 6.61 us -> none  [imaging(): columns = columns.reshape(count, FREQ, 2, COLS)]
  transfers between devices with their start and end apart: 12 -> 20, of which waited for: 9 -> 6; matrix products, arithmetic and copies ran while one was open for 2% -> 2% of each run, Pallas kernels for 0% -> 0%
where the time goes in v1:
time: 79.2 us; the launch traced here: 78.9 us
  Pallas kernels  28.2 us (36%)
  starting transfers between devices  21.9 us (28%)
  waiting for transfers between devices  16.4 us (21%)
  local copies, waits for them, and re-layouts  5.84 us (7%)
  blocking collectives  5.18 us (7%)
  between operations  0.87 us (1%)
    pallas_call x3, Pallas kernels, call(): pl.pallas_call(kernel, out_shape=out_shapes, grid_spec=pltpu.PrefetchScal...  28.2 us
    ppermute x11, starting transfers between devices, shifted(): lax.ppermute(array, axis, [(i, (i + by) % size) for i in range(size)])  20.2 us
    ppermute x11, waiting for transfers between devices, shifted(): lax.ppermute(array, axis, [(i, (i + by) % size) for i in range(size)])  15.5 us
    all_gather x1, blocking collectives, per_device(): packed = lax.all_gather(packed, 'src', axis=0, tiled=True)  5.18 us
    unnamed x50, local copies, waits for them, and re-layouts  4.22 us
    ppermute x9, starting transfers between devices, partner(): return lax.ppermute(array, 'src', [(i, i ^ 1) for i in range(size)])  1.69 us
  transfers between devices with their start and end apart: 20, of which 6 were waited for; matrix products, arithmetic and copies ran while one was open for 2% of the time, Pallas kernels for 0%

profile of v1, /device:TPU:0, one launch (start us, length us, event | category | flops | bytes accessed | tf_op | source)
XLA Modules:
  0.0 78.9 jit_solution(10193777870717989802)
XLA Ops:
  0.6 0.0 copy-start
  0.6 1.0 %fusion = (f32[64,512]{1,0:T(8,128)S(1)}, f32[64,512]{1,0:T(8,128)S(1)}) fusion(f32[128,512]{1,0:T(8,128)} %refs_12_.1), kind=kLoop, calls=%fused_computation.2 | loop fusion | bytes 524288 | tf_op jit(solution)/shard_map/slice | solution.py:316
  1.7 5.1 %collective-permute-start.1 = (f32[64,512]{1,0:T(8,128)S(1)}, f32[64,512]{1,0:T(8,128)S(1)}, u32[]{:S(2)}, u32[]{:S(2)}) collective-permute-start(f32[64,512]{1,0:T(8,128)S(1)} %get-tuple-element.14), channel_id=1, source_target_pairs={{0,12},{4,0},{8,4},{12,8},{1,13},{5,1},{9,5},{13,9},{2,14},{6,2},{... | collective-permute-start | bytes 393224 | tf_op jit(solution)/shard_map/ppermute | solution.py:34
  6.8 0.0 collective-permute-start
  6.8 0.0 copy-start.1
  6.8 0.7 copy-done.1
  7.5 0.7 copy-done.2
  8.2 5.2 %all-gather = f32[4,8,3]{1,2,0:T(4,128)S(1)} all-gather(f32[1,8,3]{1,2,0:T(4,128)S(1)} %maximum_bitcast_fusion), channel_id=1, replica_groups=mesh['band'=2,'strip'=4,'src'=4] {'src'}, dimensions={0}, use_global_device_ids=true | all-gather | bytes 480 | tf_op jit(solution)/shard_map/all_gather | solution.py:317
  13.4 0.1 reshape.9
  13.5 0.1 copy.16
  13.5 0.6 convert_element_type.10.shift_ref.refs_1_
  14.2 0.6 slice_bitcast_fusion.weight_ref.refs_2_
  14.7 0.0 copy-start.4
  14.8 0.6 copy-done.3
  15.4 0.0 copy-done.4
  15.4 10.2 %first_image.1.refs_3_ = f32[112,256]{1,0:T(8,128)} custom-call(s32[1]{0:T(128)} %bitcast.half_ref.refs_0_, s32[32,2]{1,0:T(8,128)} %convert_element_type.10.shift_ref.refs_1_, f32[32]{0:T(128)} %slice_bitcast_fusion.weight_ref.refs_2_, f32[64,512]{1,0:T(8,128)} %copy-done.4, f32[128,512]{1,0:T(8,128)} %refs_12_.1, f32[64,512]{1,0:T(8,128)} %copy-done.3, ...), custom_call_target="tpu_custom_call" | custom-call | flops 6442450944 | bytes 4194304 | tf_op jit(solution)/shard_map/first_image/pallas_call | solution.py:356
  25.7 0.1 collective-permute-start.4
  25.8 4.3 %collective-permute-start.3 = (f32[112,256]{1,0:T(8,128)}, f32[112,256]{1,0:T(8,128)S(1)}, u32[]{:S(2)}, u32[]{:S(2)}) collective-permute-start(f32[112,256]{1,0:T(8,128)} %first_image.1.refs_3_), channel_id=1, source_target_pairs={{0,8},{4,12},{8,0},{12,4},{1,9},{5,13},{9,1},{13,5},{2,10},{6,14},... | collective-permute-start | bytes 344072 | tf_op jit(solution)/shard_map/ppermute | solution.py:34
  30.1 2.1 %collective-permute-start.11 = (bf16[64,512]{1,0:T(8,128)(2,1)S(1)}, bf16[64,512]{1,0:T(8,128)(2,1)S(1)}, u32[]{:S(2)}, u32[]{:S(2)}) collective-permute-start(bf16[64,512]{1,0:T(8,128)(2,1)S(1)} %get-tuple-element.16), channel_id=1, source_target_pairs={{0,4},{4,8},{8,12},{12,0},{1,5},{5,9},{9,13},{13,1},{2,6},{6,10},{... | collective-permute-start | bytes 196616 | tf_op jit(solution)/shard_map/ppermute | solution.py:34
  32.1 1.8 %collective-permute-start.9 = (bf16[64,512]{1,0:T(8,128)(2,1)S(1)}, bf16[64,512]{1,0:T(8,128)(2,1)S(1)}, u32[]{:S(2)}, u32[]{:S(2)}) collective-permute-start(bf16[64,512]{1,0:T(8,128)(2,1)S(1)} %get-tuple-element.17), channel_id=1, source_target_pairs={{0,12},{4,0},{8,4},{12,8},{1,13},{5,1},{9,5},{13,9},{2,14},{6,2},{... | collective-permute-start | bytes 196616 | tf_op jit(solution)/shard_map/ppermute | solution.py:34
  33.9 6.2 %collective-permute-done.11.refs_16_ = bf16[64,512]{1,0:T(8,128)(2,1)S(1)} collective-permute-done((bf16[64,512]{1,0:T(8,128)(2,1)S(1)}, bf16[64,512]{1,0:T(8,128)(2,1)S(1)}, u32[]{:S(2)}, u32[]{:S(2)}) %collective-permute-start.11) | collective-permute-done | bytes 65568 | tf_op jit(solution)/shard_map/ppermute | solution.py:34
  40.1 3.0 %collective-permute-start.10 = (bf16[128,512]{1,0:T(8,128)(2,1)S(1)}, bf16[128,512]{1,0:T(8,128)(2,1)S(1)}, u32[]{:S(2)}, u32[]{:S(2)}) collective-permute-start(bf16[128,512]{1,0:T(8,128)(2,1)S(1)} %convert_element_type.11), channel_id=1, source_target_pairs={{0,8},{4,12},{8,0},{12,4},{1,9},{5,13},{9,1},{13,5},{2,10},{6,14},... | collective-permute-start | bytes 393224 | tf_op jit(solution)/shard_map/ppermute | solution.py:34
  43.1 0.0 collective-permute-done.9.refs_14_
  43.1 0.1 collective-permute-start.5
  43.2 0.5 collective-permute-start.8
  43.7 0.0 collective-permute-done.3.refs_5_
  43.7 0.1 collective-permute-start.7
  43.8 0.4 collective-permute-start.6
  44.2 5.1 %collective-permute-done.10.refs_15_ = bf16[128,512]{1,0:T(8,128)(2,1)S(1)} collective-permute-done((bf16[128,512]{1,0:T(8,128)(2,1)S(1)}, bf16[128,512]{1,0:T(8,128)(2,1)S(1)}, u32[]{:S(2)}, u32[]{:S(2)}) %collective-permute-start.10) | collective-permute-done | bytes 131104 | tf_op jit(solution)/shard_map/ppermute | solution.py:34
  49.4 0.6 copy-done.5
  49.9 0.1 copy-done.11
  50.0 0.0 copy-done.12
  50.0 0.0 copy-done.13
  50.1 0.6 copy-done.14
  50.7 13.3 %later_image.1 = (bf16[112,256]{1,0:T(8,128)(2,1)}, f32[128,256]{1,0:T(8,128)}, f32[64,512]{1,0:T(8,128)}, f32[128,512]{1,0:T(8,128)}, f32[64,512]{1,0:T(8,128)}, /*index=5*/f32[256,512]{1,0:T(8,128)}) custom-call(s32[1]{0:T(128)} %bitcast.half_ref.refs_0_, s32[32,2]{1,0:T(8,128)} %convert_element_type.10.shift_ref.refs_1_, ...), custom_call_target="tpu_custom_call" | custom-call | flops 6442450944 | bytes 4194304 | tf_op jit(solution)/shard_map/later_image/pallas_call | solution.py:356
  64.0 0.1 collective-permute-start.19
  64.2 0.0 collective-permute-start.14
  64.2 2.4 %collective-permute-start.13 = (bf16[112,256]{1,0:T(8,128)(2,1)}, bf16[112,256]{1,0:T(8,128)(2,1)S(1)}, u32[]{:S(2)}, u32[]{:S(2)}) collective-permute-start(bf16[112,256]{1,0:T(8,128)(2,1)} %get-tuple-element.8.refs_1_), channel_id=1, source_target_pairs={{0,8},{4,12},{8,0},{12,4},{1,9},{5,13},{9,1},{13,5},{2,10},{6,14},... | collective-permute-start | bytes 172040 | tf_op jit(solution)/shard_map/ppermute | solution.py:34
  66.5 1.5 %collective-permute-start.12 = (bf16[112,256]{1,0:T(8,128)(2,1)}, bf16[112,256]{1,0:T(8,128)(2,1)S(1)}, u32[]{:S(2)}, u32[]{:S(2)}) collective-permute-start(bf16[112,256]{1,0:T(8,128)(2,1)} %get-tuple-element.8.refs_1_), channel_id=1, source_target_pairs={{0,12},{4,0},{8,4},{12,8},{1,13},{5,1},{9,5},{13,9},{2,14},{6,2},{... | collective-permute-start | bytes 172040 | tf_op jit(solution)/shard_map/ppermute | solution.py:34
  68.0 3.1 %collective-permute-done.14.refs_4_ = bf16[112,256]{1,0:T(8,128)(2,1)S(1)} collective-permute-done((bf16[112,256]{1,0:T(8,128)(2,1)}, bf16[112,256]{1,0:T(8,128)(2,1)S(1)}, u32[]{:S(2)}, u32[]{:S(2)}) %collective-permute-start.14) | collective-permute-done | bytes 57376 | tf_op jit(solution)/shard_map/ppermute | solution.py:34
  71.1 1.2 %collective-permute-done.13.refs_3_ = bf16[112,256]{1,0:T(8,128)(2,1)S(1)} collective-permute-done((bf16[112,256]{1,0:T(8,128)(2,1)}, bf16[112,256]{1,0:T(8,128)(2,1)S(1)}, u32[]{:S(2)}, u32[]{:S(2)}) %collective-permute-start.13) | collective-permute-done | bytes 57376 | tf_op jit(solution)/shard_map/ppermute | solution.py:34
  72.2 0.5 collective-permute-start.16
  72.8 0.7 collective-permute-done.17.refs_7_
  73.5 0.2 collective-permute-done.16.refs_6_
  73.7 0.4 copy-done.22
  74.1 0.2 copy-done.23
  74.3 0.1 copy-done.6
  74.3 4.6 %last_step.1 = (f32[128,512]{1,0:T(8,128)}, f32[128,512]{1,0:T(8,128)}) custom-call(s32[1]{0:T(128)} %bitcast.half_ref.refs_0_, bf16[112,256]{1,0:T(8,128)(2,1)} %get-tuple-element.8.refs_1_, bf16[112,256]{1,0:T(8,128)(2,1)} %copy-done.19, bf16[112,256]{1,0:T(8,128)(2,1)} %copy-done.18, bf16[112,256]{1,0:T(8,128)(2,1)} %copy-done.17, ...), custom_call_target="tpu_custom_call" | custom-call | flops 1073741824 | bytes 4194304 | tf_op jit(solution)/shard_map/last_step/pallas_call | solution.py:356
  (55 shorter events, 0.1 us)
Async XLA Ops:
  0.6 6.2 %copy-start = (f32[128,512]{1,0:T(8,128)S(1)}, f32[128,512]{1,0:T(8,128)}, u32[]{:S(2)}) copy-start(f32[128,512]{1,0:T(8,128)} %refs_12_.1) | copy-start | bytes 786436
  1.7 13.1 %collective-permute-start.1 = (f32[64,512]{1,0:T(8,128)S(1)}, f32[64,512]{1,0:T(8,128)S(1)}, u32[]{:S(2)}, u32[]{:S(2)}) collective-permute-start(f32[64,512]{1,0:T(8,128)S(1)} %get-tuple-element.14), channel_id=1, source_target_pairs={{0,12},{4,0},{8,4},{12,8},{1,13},{5,1},{9,5},{13,9},{2,14},{6,2},{... | collective-permute-start | bytes 393224 | tf_op jit(solution)/shard_map/ppermute | solution.py:34
  6.8 7.9 %collective-permute-start = (f32[64,512]{1,0:T(8,128)S(1)}, f32[64,512]{1,0:T(8,128)S(1)}, u32[]{:S(2)}, u32[]{:S(2)}) collective-permute-start(f32[64,512]{1,0:T(8,128)S(1)} %get-tuple-element.15), channel_id=1, source_target_pairs={{0,4},{4,8},{8,12},{12,0},{1,5},{5,9},{9,13},{13,1},{2,6},{6,10},{... | collective-permute-start | bytes 393224 | tf_op jit(solution)/shard_map/ppermute | solution.py:34
  6.8 0.7 copy-start.1
  7.5 0.7 copy-start.2
  14.7 0.7 copy-start.3
  14.7 0.7 copy-start.4
  25.7 17.4 %copy-start.7 = (f32[112,256]{1,0:T(8,128)S(1)}, f32[112,256]{1,0:T(8,128)}, u32[]{:S(2)}) copy-start(f32[112,256]{1,0:T(8,128)} %first_image.1.refs_3_) | copy-start | bytes 344068
  25.7 17.5 %collective-permute-start.4 = (f32[112,256]{1,0:T(8,128)}, f32[112,256]{1,0:T(8,128)S(1)}, u32[]{:S(2)}, u32[]{:S(2)}) collective-permute-start(f32[112,256]{1,0:T(8,128)} %first_image.1.refs_3_), channel_id=1, source_target_pairs={{0,4},{4,8},{8,12},{12,0},{1,5},{5,9},{9,13},{13,1},{2,6},{6,10},{... | collective-permute-start | bytes 344072 | tf_op jit(solution)/shard_map/ppermute | solution.py:34
  25.8 17.9 %collective-permute-start.3 = (f32[112,256]{1,0:T(8,128)}, f32[112,256]{1,0:T(8,128)S(1)}, u32[]{:S(2)}, u32[]{:S(2)}) collective-permute-start(f32[112,256]{1,0:T(8,128)} %first_image.1.refs_3_), channel_id=1, source_target_pairs={{0,8},{4,12},{8,0},{12,4},{1,9},{5,13},{9,1},{13,5},{2,10},{6,14},... | collective-permute-start | bytes 344072 | tf_op jit(solution)/shard_map/ppermute | solution.py:34
  30.1 13.7 %collective-permute-start.2 = (f32[112,256]{1,0:T(8,128)}, f32[112,256]{1,0:T(8,128)S(1)}, u32[]{:S(2)}, u32[]{:S(2)}) collective-permute-start(f32[112,256]{1,0:T(8,128)} %first_image.1.refs_3_), channel_id=1, source_target_pairs={{0,12},{4,0},{8,4},{12,8},{1,13},{5,1},{9,5},{13,9},{2,14},{6,2},{... | collective-permute-start | bytes 344072 | tf_op jit(solution)/shard_map/ppermute | solution.py:34
  30.1 10.1 %collective-permute-start.11 = (bf16[64,512]{1,0:T(8,128)(2,1)S(1)}, bf16[64,512]{1,0:T(8,128)(2,1)S(1)}, u32[]{:S(2)}, u32[]{:S(2)}) collective-permute-start(bf16[64,512]{1,0:T(8,128)(2,1)S(1)} %get-tuple-element.16), channel_id=1, source_target_pairs={{0,4},{4,8},{8,12},{12,0},{1,5},{5,9},{9,13},{13,1},{2,6},{6,10},{... | collective-permute-start | bytes 196616 | tf_op jit(solution)/shard_map/ppermute | solution.py:34
  32.1 11.0 %collective-permute-start.9 = (bf16[64,512]{1,0:T(8,128)(2,1)S(1)}, bf16[64,512]{1,0:T(8,128)(2,1)S(1)}, u32[]{:S(2)}, u32[]{:S(2)}) collective-permute-start(bf16[64,512]{1,0:T(8,128)(2,1)S(1)} %get-tuple-element.17), channel_id=1, source_target_pairs={{0,12},{4,0},{8,4},{12,8},{1,13},{5,1},{9,5},{13,9},{2,14},{6,2},{... | collective-permute-start | bytes 196616 | tf_op jit(solution)/shard_map/ppermute | solution.py:34
  40.1 9.2 %copy-start.15 = (bf16[64,512]{1,0:T(8,128)(2,1)}, bf16[64,512]{1,0:T(8,128)(2,1)S(1)}, u32[]{:S(2)}) copy-start(bf16[64,512]{1,0:T(8,128)(2,1)S(1)} %collective-permute-done.11.refs_16_) | copy-start | bytes 196612
  40.1 9.1 %collective-permute-start.10 = (bf16[128,512]{1,0:T(8,128)(2,1)S(1)}, bf16[128,512]{1,0:T(8,128)(2,1)S(1)}, u32[]{:S(2)}, u32[]{:S(2)}) collective-permute-start(bf16[128,512]{1,0:T(8,128)(2,1)S(1)} %convert_element_type.11), channel_id=1, source_target_pairs={{0,8},{4,12},{8,0},{12,4},{1,9},{5,13},{9,1},{13,5},{2,10},{6,14},... | collective-permute-start | bytes 393224 | tf_op jit(solution)/shard_map/ppermute | solution.py:34
  43.1 6.2 %copy-start.16 = (bf16[64,512]{1,0:T(8,128)(2,1)}, bf16[64,512]{1,0:T(8,128)(2,1)S(1)}, u32[]{:S(2)}) copy-start(bf16[64,512]{1,0:T(8,128)(2,1)S(1)} %collective-permute-done.9.refs_14_) | copy-start | bytes 196612
  43.1 6.2 %collective-permute-start.5 = (f32[112,256]{1,0:T(8,128)S(1)}, f32[112,256]{1,0:T(8,128)S(1)}, u32[]{:S(2)}, u32[]{:S(2)}) collective-permute-start(f32[112,256]{1,0:T(8,128)S(1)} %copy-done.7), channel_id=1, source_target_pairs={{0,1},{1,0},{2,3},{3,2},{4,5},{5,4},{6,7},{7,6},{8,9},{9,8},{10,11... | collective-permute-start | bytes 344072 | tf_op jit(solution)/shard_map/ppermute | solution.py:39
  43.2 6.1 %copy-start.8 = (f32[112,256]{1,0:T(8,128)}, f32[112,256]{1,0:T(8,128)S(1)}, u32[]{:S(2)}) copy-start(f32[112,256]{1,0:T(8,128)S(1)} %collective-permute-done.4.refs_6_) | copy-start | bytes 344068
  43.2 6.1 %collective-permute-start.8 = (f32[112,256]{1,0:T(8,128)S(1)}, f32[112,256]{1,0:T(8,128)S(1)}, u32[]{:S(2)}, u32[]{:S(2)}) collective-permute-start(f32[112,256]{1,0:T(8,128)S(1)} %collective-permute-done.4.refs_6_), channel_id=1, source_target_pairs={{0,1},{1,0},{2,3},{3,2},{4,5},{5,4},{6,7},{7,6},{8,9},{9,8},{10,11... | collective-permute-start | bytes 344072 | tf_op jit(solution)/shard_map/ppermute | solution.py:39
  43.7 5.7 %copy-start.9 = (f32[112,256]{1,0:T(8,128)}, f32[112,256]{1,0:T(8,128)S(1)}, u32[]{:S(2)}) copy-start(f32[112,256]{1,0:T(8,128)S(1)} %collective-permute-done.3.refs_5_) | copy-start | bytes 344068
  43.7 5.6 %collective-permute-start.7 = (f32[112,256]{1,0:T(8,128)S(1)}, f32[112,256]{1,0:T(8,128)S(1)}, u32[]{:S(2)}, u32[]{:S(2)}) collective-permute-start(f32[112,256]{1,0:T(8,128)S(1)} %collective-permute-done.3.refs_5_), channel_id=1, source_target_pairs={{0,1},{1,0},{2,3},{3,2},{4,5},{5,4},{6,7},{7,6},{8,9},{9,8},{10,11... | collective-permute-start | bytes 344072 | tf_op jit(solution)/shard_map/ppermute | solution.py:39
  43.8 5.6 %copy-start.10 = (f32[112,256]{1,0:T(8,128)}, f32[112,256]{1,0:T(8,128)S(1)}, u32[]{:S(2)}) copy-start(f32[112,256]{1,0:T(8,128)S(1)} %collective-permute-done.2.refs_4_) | copy-start | bytes 344068
  43.8 5.5 %collective-permute-start.6 = (f32[112,256]{1,0:T(8,128)S(1)}, f32[112,256]{1,0:T(8,128)S(1)}, u32[]{:S(2)}, u32[]{:S(2)}) collective-permute-start(f32[112,256]{1,0:T(8,128)S(1)} %collective-permute-done.2.refs_4_), channel_id=1, source_target_pairs={{0,1},{1,0},{2,3},{3,2},{4,5},{5,4},{6,7},{7,6},{8,9},{9,8},{10,11... | collective-permute-start | bytes 344072 | tf_op jit(solution)/shard_map/ppermute | solution.py:39
  49.3 0.7 copy-start.5
  49.3 0.7 copy-start.11
  49.3 0.8 copy-start.12
  49.3 0.8 copy-start.13
  50.1 0.6 copy-start.14
  64.0 9.6 %collective-permute-start.19 = (f32[128,256]{1,0:T(8,128)}, f32[128,256]{1,0:T(8,128)S(1)}, u32[]{:S(2)}, u32[]{:S(2)}) collective-permute-start(f32[128,256]{1,0:T(8,128)} %get-tuple-element.13.refs_15_), channel_id=1, source_target_pairs={{0,1},{1,0},{2,3},{3,2},{4,5},{5,4},{6,7},{7,6},{8,9},{9,8},{10,11... | collective-permute-start | bytes 393224 | tf_op jit(solution)/shard_map/ppermute | solution.py:39
  64.2 6.9 %collective-permute-start.14 = (bf16[112,256]{1,0:T(8,128)(2,1)}, bf16[112,256]{1,0:T(8,128)(2,1)S(1)}, u32[]{:S(2)}, u32[]{:S(2)}) collective-permute-start(bf16[112,256]{1,0:T(8,128)(2,1)} %get-tuple-element.8.refs_1_), channel_id=1, source_target_pairs={{0,4},{4,8},{8,12},{12,0},{1,5},{5,9},{9,13},{13,1},{2,6},{6,10},{... | collective-permute-start | bytes 172040 | tf_op jit(solution)/shard_map/ppermute | solution.py:34
  64.2 8.0 %collective-permute-start.13 = (bf16[112,256]{1,0:T(8,128)(2,1)}, bf16[112,256]{1,0:T(8,128)(2,1)S(1)}, u32[]{:S(2)}, u32[]{:S(2)}) collective-permute-start(bf16[112,256]{1,0:T(8,128)(2,1)} %get-tuple-element.8.refs_1_), channel_id=1, source_target_pairs={{0,8},{4,12},{8,0},{12,4},{1,9},{5,13},{9,1},{13,5},{2,10},{6,14},... | collective-permute-start | bytes 172040 | tf_op jit(solution)/shard_map/ppermute | solution.py:34
  66.5 5.7 %collective-permute-start.12 = (bf16[112,256]{1,0:T(8,128)(2,1)}, bf16[112,256]{1,0:T(8,128)(2,1)S(1)}, u32[]{:S(2)}, u32[]{:S(2)}) collective-permute-start(bf16[112,256]{1,0:T(8,128)(2,1)} %get-tuple-element.8.refs_1_), channel_id=1, source_target_pairs={{0,12},{4,0},{8,4},{12,8},{1,13},{5,1},{9,5},{13,9},{2,14},{6,2},{... | collective-permute-start | bytes 172040 | tf_op jit(solution)/shard_map/ppermute | solution.py:34
  68.0 4.8 %collective-permute-start.15 = (bf16[112,256]{1,0:T(8,128)(2,1)}, bf16[112,256]{1,0:T(8,128)(2,1)S(1)}, u32[]{:S(2)}, u32[]{:S(2)}) collective-permute-start(bf16[112,256]{1,0:T(8,128)(2,1)} %get-tuple-element.8.refs_1_), channel_id=1, source_target_pairs={{0,1},{1,0},{2,3},{3,2},{4,5},{5,4},{6,7},{7,6},{8,9},{9,8},{10,11... | collective-permute-start | bytes 172040 | tf_op jit(solution)/shard_map/ppermute | solution.py:39
  71.1 2.6 %copy-start.17 = (bf16[112,256]{1,0:T(8,128)(2,1)}, bf16[112,256]{1,0:T(8,128)(2,1)S(1)}, u32[]{:S(2)}) copy-start(bf16[112,256]{1,0:T(8,128)(2,1)S(1)} %collective-permute-done.14.refs_4_) | copy-start | bytes 172036
  71.1 1.7 %collective-permute-start.18 = (bf16[112,256]{1,0:T(8,128)(2,1)S(1)}, bf16[112,256]{1,0:T(8,128)(2,1)S(1)}, u32[]{:S(2)}, u32[]{:S(2)}) collective-permute-start(bf16[112,256]{1,0:T(8,128)(2,1)S(1)} %collective-permute-done.14.refs_4_), channel_id=1, source_target_pairs={{0,1},{1,0},{2,3},{3,2},{4,5},{5,4},{6,7},{7,6},{8,9},{9,8},{10,11... | collective-permute-start | bytes 172040 | tf_op jit(solution)/shard_map/ppermute | solution.py:39
  72.2 1.4 %copy-start.18 = (bf16[112,256]{1,0:T(8,128)(2,1)}, bf16[112,256]{1,0:T(8,128)(2,1)S(1)}, u32[]{:S(2)}) copy-start(bf16[112,256]{1,0:T(8,128)(2,1)S(1)} %collective-permute-done.13.refs_3_) | copy-start | bytes 172036
  72.2 1.2 %collective-permute-start.17 = (bf16[112,256]{1,0:T(8,128)(2,1)S(1)}, bf16[112,256]{1,0:T(8,128)(2,1)S(1)}, u32[]{:S(2)}, u32[]{:S(2)}) collective-permute-start(bf16[112,256]{1,0:T(8,128)(2,1)S(1)} %collective-permute-done.13.refs_3_), channel_id=1, source_target_pairs={{0,1},{1,0},{2,3},{3,2},{4,5},{5,4},{6,7},{7,6},{8,9},{9,8},{10,11... | collective-permute-start | bytes 172040 | tf_op jit(solution)/shard_map/ppermute | solution.py:39
  72.2 1.4 %copy-start.19 = (bf16[112,256]{1,0:T(8,128)(2,1)}, bf16[112,256]{1,0:T(8,128)(2,1)S(1)}, u32[]{:S(2)}) copy-start(bf16[112,256]{1,0:T(8,128)(2,1)S(1)} %collective-permute-done.12.refs_2_) | copy-start | bytes 172036
  72.2 1.4 %collective-permute-start.16 = (bf16[112,256]{1,0:T(8,128)(2,1)S(1)}, bf16[112,256]{1,0:T(8,128)(2,1)S(1)}, u32[]{:S(2)}, u32[]{:S(2)}) collective-permute-start(bf16[112,256]{1,0:T(8,128)(2,1)S(1)} %collective-permute-done.12.refs_2_), channel_id=1, source_target_pairs={{0,1},{1,0},{2,3},{3,2},{4,5},{5,4},{6,7},{7,6},{8,9},{9,8},{10,11... | collective-permute-start | bytes 172040 | tf_op jit(solution)/shard_map/ppermute | solution.py:39
  72.7 0.9 %copy-start.20 = (bf16[112,256]{1,0:T(8,128)(2,1)}, bf16[112,256]{1,0:T(8,128)(2,1)S(1)}, u32[]{:S(2)}) copy-start(bf16[112,256]{1,0:T(8,128)(2,1)S(1)} %collective-permute-done.15.refs_5_) | copy-start | bytes 172036
  72.7 0.9 %copy-start.21 = (bf16[112,256]{1,0:T(8,128)(2,1)}, bf16[112,256]{1,0:T(8,128)(2,1)S(1)}, u32[]{:S(2)}) copy-start(bf16[112,256]{1,0:T(8,128)(2,1)S(1)} %collective-permute-done.18.refs_8_) | copy-start | bytes 172036
  73.5 0.6 copy-start.22
  73.6 0.6 copy-start.23
  73.6 0.7 copy-start.6

commit v2 on v1

v2 whole, which is shorter than its diff:
```python
import functools
import math

import jax
import jax.numpy as jnp
import numpy as np
from jax import lax
from jax.experimental import pallas as pl
from jax.experimental.pallas import tpu as pltpu
from jax.sharding import PartitionSpec as P

HALO = 64
FREQ = 128
ITERS = 2

steepness = 20.0
dose_level = 0.27
step_size = 1.0
epsilon = 1e-06

RADIUS = FREQ // 4
MAX_SHIFT = FREQ // 8
LOW = FREQ // 2 - RADIUS - MAX_SHIFT
KEEP = FREQ - LOW
ALIGN = 16
SPAN = 2 * RADIUS + ALIGN
VARIANTS = 2 * MAX_SHIFT // ALIGN + 1
SPLIT = 2
GROUP = 16
STEP = 8


def shifted(array, axis, by):
    size = lax.axis_size(axis)
    return lax.ppermute(array, axis, [(i, (i + by) % size) for i in range(size)])


def partner(array):
    size = lax.axis_size("src")
    return lax.ppermute(array, "src", [(i, i ^ 1) for i in range(size)])


def phase_pair(freq_ids, points, period):
    index = freq_ids[:, None] % period * points[None, :] % period
    angle = np.float32(2.0 * math.pi / period) * index.astype(np.float32)
    return (np.cos(angle), np.sin(angle))


@functools.lru_cache(maxsize=None)
def build_tables(rows, cols):
    low = jnp.bfloat16
    freq_ids = np.arange(FREQ, dtype=np.int32) - FREQ // 2
    win_len = rows + 2 * HALO
    row_cos, row_sin = phase_pair(freq_ids, np.arange(win_len, dtype=np.int32), win_len)
    forward_rows = (np.concatenate([row_cos, -row_sin], 0) / np.float32(win_len)).astype(low)
    col_cos, col_sin = phase_pair(freq_ids, np.arange(cols, dtype=np.int32), cols)
    real_part = np.concatenate([col_cos.T, -col_sin.T], 1) / np.float32(cols)
    imag_part = np.concatenate([col_sin.T, col_cos.T], 1) / np.float32(cols)
    forward_cols = np.stack([real_part, imag_part], 0).astype(low)
    halves = []
    for part in range(SPLIT):
        at = slice(part * cols // SPLIT, (part + 1) * cols // SPLIT)
        halves.append(
            np.concatenate(
                [
                    np.concatenate([col_cos[:, at], col_sin[:, at]], 1),
                    np.concatenate([-col_sin[:, at], col_cos[:, at]], 1),
                ],
                0,
            )
        )
    inverse_cols = np.stack(halves, 0).astype(low)
    inner_cos, inner_sin = phase_pair(freq_ids, np.arange(rows, dtype=np.int32) + HALO, win_len)
    inner_cos, inner_sin = (inner_cos.T, inner_sin.T)
    inverse_rows = np.stack(
        [np.stack([inner_cos, -inner_sin], 1), np.stack([inner_sin, inner_cos], 1)], 0
    ).astype(low)
    windows = np.stack(
        [
            inverse_rows[:, :, :, LOW + v * ALIGN : LOW + v * ALIGN + SPAN].reshape(2 * rows, 2 * SPAN)
            for v in range(VARIANTS)
        ],
        0,
    )
    inverse_rows_t = inverse_rows.transpose(2, 3, 0, 1).reshape(2 * FREQ, 2 * rows)
    return (forward_rows, np.ascontiguousarray(forward_rows.T), forward_cols, inverse_cols, windows, np.ascontiguousarray(inverse_rows_t))


def dot(a, b):
    return jnp.dot(a, b, preferred_element_type=jnp.float32)


def dot_t(a, b):
    return lax.dot_general(a, b, (((1,), (1,)), ((), ())), preferred_element_type=jnp.float32)


def read_sources(packs, at_ref, weight_ref):
    per = packs[0].shape[0] // 3
    for d, pack in enumerate(packs):
        for i in range(per):
            s = d * per + i
            along_k = pack[2 * i].astype(jnp.int32)
            first = FREQ // 2 - RADIUS - along_k
            at_ref[0, s] = first - lax.rem(first, ALIGN)
            at_ref[1, s] = along_k - FREQ // 2
            at_ref[2, s] = pack[2 * i + 1].astype(jnp.int32) - FREQ // 2
            weight_ref[s] = pack[2 * per + i]


def window_of(at_ref, s):
    return pl.multiple_of(at_ref[0, s], ALIGN)


def image(mask, shift_ref, weight_ref, tables, target_ref, partial_ref, resist_ref, scratch, rows):
    fr_ref, fc_ref, gc_ref, grw_ref, grt_ref = tables
    spec_ref, pupil_ref, cols_ref, field_ref, dcols_ref, inten_ref, acc_ref = scratch
    sources = field_ref.shape[0]
    width = field_ref.shape[2]
    half = dot(fr_ref[...], mask).astype(jnp.bfloat16)
    spectrum = dot(half[:FREQ], fc_ref[0]) + dot(half[FREQ:], fc_ref[1])
    spec_ref[...] = spectrum.astype(jnp.bfloat16).astype(jnp.float32)
    inten_ref[...] = jnp.zeros_like(inten_ref)
    acc_ref[...] = jnp.zeros_like(acc_ref)

    def to_columns(g, carry):
        pieces = []
        for i in range(GROUP):
            s = g * GROUP + i
            base = window_of(shift_ref, s)
            along_k = lax.broadcasted_iota(jnp.int32, (SPAN, FREQ), 0) + (base + shift_ref[1, s])
            along_l = lax.broadcasted_iota(jnp.int32, (SPAN, FREQ), 1) + shift_ref[2, s]
            inside = along_k * along_k + along_l * along_l <= RADIUS * RADIUS
            pupil = jnp.where(inside, 1.0, 0.0)
            pupil_ref[s] = pupil
            part = spec_ref[pl.ds(base, SPAN), :]
            pieces.append((part * jnp.concatenate([pupil, pupil], 1)).astype(jnp.bfloat16))
        out = dot(jnp.concatenate(pieces, 0), gc_ref[...]).astype(jnp.bfloat16)
        for i in range(GROUP):
            s = g * GROUP + i
            cols_ref[s, :SPAN, :] = out[i * SPAN : (i + 1) * SPAN, :width]
            cols_ref[s, SPAN:, :] = out[i * SPAN : (i + 1) * SPAN, width:]
        return carry

    lax.fori_loop(0, sources // GROUP, to_columns, 0)

    def to_field(g, carry):
        total = inten_ref[...]
        for i in range(STEP):
            s = g * STEP + i
            variant = lax.div(shift_ref[0, s] - LOW, ALIGN)
            field = dot(grw_ref[variant], cols_ref[s])
            field_ref[s] = field
            scaled = weight_ref[s] * (1.0 / sources)
            total = total + scaled * (field[:rows] * field[:rows] + field[rows:] * field[rows:])
        inten_ref[...] = total
        return carry

    lax.fori_loop(0, sources // STEP, to_field, 0)

    resist = jax.nn.sigmoid(steepness * (inten_ref[...] - dose_level))
    if resist_ref is not None:
        resist_ref[...] = resist
    goal = target_ref[...].astype(jnp.float32)
    inten_ref[...] = 2.0 * (resist - goal) * steepness * resist * (1.0 - resist)

    def to_d_columns(g, carry):
        d_int = inten_ref[...]
        for i in range(STEP):
            s = g * STEP + i
            base = window_of(shift_ref, s)
            scale = d_int * (2.0 * weight_ref[s] * (1.0 / sources))
            d_field = (field_ref[s] * jnp.concatenate([scale, scale], 0)).astype(jnp.bfloat16)
            table = jnp.concatenate([grt_ref[pl.ds(base, SPAN), :], grt_ref[pl.ds(base + FREQ, SPAN), :]], 0)
            d_cols = dot(table, d_field).astype(jnp.bfloat16)
            dcols_ref[s, :, :width] = d_cols[:SPAN]
            dcols_ref[s, :, width:] = d_cols[SPAN:]
        return carry

    lax.fori_loop(0, sources // STEP, to_d_columns, 0)

    def to_d_spectrum(g, carry):
        d_cols = dcols_ref[pl.ds(g * GROUP, GROUP)].reshape(GROUP * SPAN, 2 * width)
        d_passed = dot_t(d_cols, gc_ref[...])
        for i in range(GROUP):
            s = g * GROUP + i
            base = window_of(shift_ref, s)
            pupil = pupil_ref[s]
            part = d_passed[i * SPAN : (i + 1) * SPAN] * jnp.concatenate([pupil, pupil], 1)
            acc_ref[pl.ds(base, SPAN), :] = acc_ref[pl.ds(base, SPAN), :] + part
        return carry

    lax.fori_loop(0, sources // GROUP, to_d_spectrum, 0)
    partial_ref[...] = acc_ref[LOW:, :].astype(partial_ref.dtype)


def d_windows(sums, half, fc_ref, frt_ref, dhi_ref, dlo_ref, field_ref, count):
    width = field_ref.shape[2]
    zero = jnp.zeros((LOW, 2 * FREQ), jnp.bfloat16)

    def one(o, total):
        total = total.astype(jnp.float32)
        high = total.astype(jnp.bfloat16)
        rest = (total - high.astype(jnp.float32)).astype(jnp.bfloat16)
        high = jnp.concatenate([zero, high], 0)
        rest = jnp.concatenate([zero, rest], 0)
        for p in range(2):
            d_half = dot_t(high, fc_ref[p]) + dot_t(rest, fc_ref[p])
            d_high = d_half.astype(jnp.bfloat16)
            dhi_ref[o, p * FREQ : (p + 1) * FREQ, :] = d_high
            dlo_ref[o, p * FREQ : (p + 1) * FREQ, :] = (d_half - d_high.astype(jnp.float32)).astype(jnp.bfloat16)

    one(0, sums[0][...])
    for (low, high), mine, other in zip(pairs_of(count), sums[1::2], sums[2::2]):
        if low == high:
            first = jnp.where(half == 0, mine[...], other[...])
            second = jnp.where(half == 0, other[...], mine[...])
            one(low, jnp.concatenate([first, second], 0))
        else:
            one(jnp.where(half == 0, low, high), mine[...])
            one(jnp.where(half == 0, high, low), other[...])
    for o in range(count):
        d_win = dot(frt_ref[...], dhi_ref[o]) + dot(frt_ref[...], dlo_ref[o])
        for h in range(SPLIT):
            field_ref[SPLIT * o + h] = d_win[:, h * width : (h + 1) * width]


def d_block(field_ref, i, count, rows):
    prev = (i - 1) % count
    return jnp.concatenate(
        [field_ref[SPLIT * i + h, :rows, :] + field_ref[SPLIT * prev + h, rows:, :] for h in range(SPLIT)], 1
    )


def put_block(field_ref, i, rows, value):
    width = field_ref.shape[2]
    for h in range(SPLIT):
        field_ref[SPLIT * i + h, :rows, :] = value[:, h * width : (h + 1) * width]


def get_block(field_ref, i, rows):
    return jnp.concatenate([field_ref[SPLIT * i + h, :rows, :] for h in range(SPLIT)], 1)


def gradients(blocks, field_ref, rows, cols):
    count = len(blocks)
    squares = jnp.zeros((1, 1), jnp.float32)
    for i, block in enumerate(blocks):
        m = jax.nn.sigmoid(block())
        d_theta = d_block(field_ref, i, count, rows) * m * (1.0 - m)
        put_block(field_ref, i, rows, d_theta)
        squares = squares + jnp.sum(d_theta * d_theta, axis=(0, 1), keepdims=True)
    return step_size * lax.rsqrt(squares / (rows * count * cols) + epsilon)


def blocks_of(state_refs, rows):
    pieces = [(ref, at) for ref in state_refs for at in range(0, ref.shape[0], HALO)]
    per = rows // HALO

    def load(i):
        return jnp.concatenate(
            [ref[at : at + HALO, :].astype(jnp.float32) for ref, at in pieces[i * per : (i + 1) * per]], 0
        )

    return [functools.partial(load, i) for i in range(len(pieces) // per)]


def first_kernel(n_packs, *refs):
    half_ref, packs, refs = refs[0], refs[1 : 1 + n_packs], refs[1 + n_packs :]
    mine_ref, other_ref, own_ref, target_ref = refs[:4]
    fr_ref, fc_ref, gc_ref, grw_ref, grt_ref, partial_ref, at_ref, weight_ref = refs[4:12]
    scratch = refs[12:]
    rows = own_ref.shape[0]
    read_sources(packs, at_ref, weight_ref)
    first = half_ref[0] == 0
    mine, other = mine_ref[...], other_ref[...]
    theta = jnp.concatenate([jnp.where(first, mine, other), own_ref[...], jnp.where(first, other, mine)], 0)
    mask = jax.nn.sigmoid(theta).astype(jnp.bfloat16)
    image(mask, at_ref, weight_ref, (fr_ref, fc_ref, gc_ref, grw_ref, grt_ref), target_ref, partial_ref, None, scratch, rows)


def later_kernel(count, n_packs, n_sums, n_state, gathered, *refs):
    half_ref, packs, refs = refs[0], refs[1 : 1 + n_packs], refs[1 + n_packs :]
    sums, state, refs = refs[:n_sums], refs[n_sums : n_sums + n_state], refs[n_sums + n_state :]
    target_ref, fr_ref, frt_ref, fc_ref, gc_ref, grw_ref, grt_ref = refs[:7]
    partial_ref, resist_ref, window_out, rest_out = refs[7:11]
    at_ref, weight_ref = refs[11:13]
    scratch, (dhi_ref, dlo_ref, band_ref) = refs[13:20], refs[20:]
    field_ref = scratch[3]
    rows, cols = window_out.shape[0] // 2, window_out.shape[1]
    half = half_ref[0]
    read_sources(packs, at_ref, weight_ref)
    if gathered:
        blocks = blocks_of(state, rows)
    else:
        place_state(state, half, band_ref, count, rows)
        blocks = blocks_of([band_ref], rows)
    d_windows(sums, half, fc_ref, frt_ref, dhi_ref, dlo_ref, field_ref, count)
    factor = gradients(blocks, field_ref, rows, cols)
    masks = []
    for i, block in enumerate(blocks):
        theta = block() - get_block(field_ref, i, rows) * factor
        if i < 2:
            window_out[i * rows : (i + 1) * rows, :] = theta
            masks.append(jax.nn.sigmoid(theta).astype(jnp.bfloat16))
        else:
            rest_out[(i - 2) * rows : (i - 1) * rows, :] = theta
    image(jnp.concatenate(masks, 0), at_ref, weight_ref, (fr_ref, fc_ref, gc_ref, grw_ref, grt_ref), target_ref, partial_ref, resist_ref, scratch, rows)


def place_state(state, half, band_ref, count, rows):
    own_ref, pieces = state[0], state[1:]
    band_ref[HALO : HALO + rows, :] = own_ref[...]
    whole = count * rows

    def put(first_row, second_row, mine, other):
        a = pl.multiple_of(jnp.where(half == 0, first_row, second_row), HALO)
        b = pl.multiple_of(jnp.where(half == 0, second_row, first_row), HALO)
        band_ref[pl.ds(a, HALO), :] = mine[...].astype(jnp.float32)
        band_ref[pl.ds(b, HALO), :] = other[...].astype(jnp.float32)

    put(0, HALO + rows, pieces[0], pieces[1])
    put(2 * rows, whole - HALO, pieces[2], pieces[3])
    for k, o in enumerate(range(2, count - 1)):
        put(HALO + o * rows, 2 * HALO + o * rows, pieces[4 + 2 * k], pieces[5 + 2 * k])


def last_kernel(count, n_sums, *refs):
    half_ref, refs = refs[0], refs[1:]
    sums, state, refs = refs[:n_sums], refs[n_sums : n_sums + 2], refs[n_sums + 2 :]
    fc_ref, frt_ref, resist_ref, resist_other, theta_out, resist_out, field_ref, dhi_ref, dlo_ref = refs
    rows, cols = theta_out.shape
    width = resist_ref.shape[1]
    half = half_ref[0]
    d_windows(sums, half, fc_ref, frt_ref, dhi_ref, dlo_ref, field_ref, count)
    factor = gradients(blocks_of(state, rows), field_ref, rows, cols)
    d_own = jnp.concatenate([get_block(field_ref, 0, rows)[HALO:], get_block(field_ref, 1, rows)[: rows - HALO]], 0)
    theta_out[...] = state[0][HALO : HALO + rows, :] - d_own * factor
    first = half == 0
    resist_out[:, :width] = jnp.where(first, resist_ref[...], resist_other[...])
    resist_out[:, width:] = jnp.where(first, resist_other[...], resist_ref[...])


def pairs_of(count):
    return [(o, count - o) for o in range(1, (count + 1) // 2)] + [(count // 2, count // 2)] * (count % 2 == 0)


def fetch(array, low, high):
    strips, size = lax.axis_size("strip"), lax.axis_size("src")
    steps = [
        (z * size + s, (z - (high if s % SPLIT else low)) % strips * size + s)
        for z in range(strips)
        for s in range(size)
    ]
    return lax.ppermute(array, ("strip", "src"), steps)


def exchange(partial, half, dtype):
    total = (partial + partner(partial)).astype(dtype)
    rows = total.shape[0] // 2
    sums = [total]
    for low, high in pairs_of(lax.axis_size("strip")):
        send = total
        if low == high:
            send = jnp.where(half == 0, total[:rows], total[rows:])
        mine = fetch(send, low, high)
        sums += [mine, partner(mine)]
    return sums


def per_device(theta, target, source_shift, source_weight):
    rows, cols = theta.shape
    count = lax.axis_size("strip")
    n_src = lax.axis_size("src")
    width = cols // SPLIT
    sources = source_weight.shape[0] * n_src
    half = (lax.axis_index("src") % SPLIT).astype(jnp.int32)
    forward_rows, forward_rows_t, forward_cols, inverse_cols, windows, inverse_rows_t = [
        jnp.asarray(t) for t in build_tables(rows, cols)
    ]
    inverse_cols = lax.dynamic_index_in_dim(inverse_cols, half, 0, keepdims=False)
    target = lax.dynamic_slice_in_dim(target, half * width, width, 1)

    even = half == 0
    head, tail = theta[:HALO], theta[rows - HALO :]
    mine = fetch(jnp.where(even, tail, head), count - 1, 1)
    pack = jnp.concatenate([source_shift.reshape(-1).astype(jnp.float32), source_weight])
    packs = [pack] + [shifted(pack, "src", k) for k in range(1, n_src)]
    pieces = [mine, partner(mine)]
    low = jnp.where(even, tail, head).astype(jnp.bfloat16)
    mine = fetch(low, 1, count - 1)
    pieces += [mine, partner(mine)]
    low = jnp.where(even, head, tail).astype(jnp.bfloat16)
    for o in range(2, count - 1):
        mine = fetch(low, o, o)
        pieces += [mine, partner(mine)]

    vmem = pl.BlockSpec(memory_space=pltpu.VMEM)
    smem = pl.BlockSpec(memory_space=pltpu.SMEM)
    f32 = jnp.float32
    source_scratch = [pltpu.SMEM((3, sources), jnp.int32), pltpu.SMEM((sources,), f32)]
    image_scratch = [
        pltpu.VMEM((FREQ, 2 * FREQ), f32),
        pltpu.VMEM((sources, SPAN, FREQ), f32),
        pltpu.VMEM((sources, 2 * SPAN, width), jnp.bfloat16),
        pltpu.VMEM((sources, 2 * rows, width), f32),
        pltpu.VMEM((sources, SPAN, 2 * width), jnp.bfloat16),
        pltpu.VMEM((rows, width), f32),
        pltpu.VMEM((FREQ, 2 * FREQ), f32),
    ]
    adjoint_scratch = [pltpu.VMEM((count, 2 * FREQ, cols), jnp.bfloat16)] * 2
    band_scratch = [pltpu.VMEM((count * rows, cols), f32)]

    def call(kernel, n_smem, args, outs, scratch, flops, name):
        held = sum(math.prod(a.shape) * a.dtype.itemsize for a in [*args, *outs])
        held += sum(math.prod(a.shape) * jnp.dtype(a.dtype).itemsize for a in scratch)
        return pl.pallas_call(
            kernel,
            out_shape=outs,
            in_specs=[smem] * n_smem + [vmem] * (len(args) - n_smem),
            out_specs=[vmem] * len(outs),
            scratch_shapes=scratch,
            compiler_params=pltpu.CompilerParams(vmem_limit_bytes=held + (6 << 20)),
            cost_estimate=pl.CostEstimate(flops=flops, bytes_accessed=4 << 20, transcendentals=1 << 20),
            name=name,
        )(*args)

    smalls = [half.reshape(1), *packs]
    partial_shape = jax.ShapeDtypeStruct((KEEP, 2 * FREQ), f32)
    image_tables = [forward_cols, inverse_cols, windows, inverse_rows_t]
    (partial,) = call(
        functools.partial(first_kernel, n_src),
        len(smalls),
        [*smalls, *pieces[:2], theta, target, forward_rows, *image_tables],
        [partial_shape],
        source_scratch + image_scratch,
        6 << 30,
        "first_image",
    )
    state, gathered = [theta, *pieces], False
    for _ in range(ITERS - 1):
        sums = exchange(partial, half, f32)
        partial, resist, *state = call(
            functools.partial(later_kernel, count, n_src, len(sums), len(state), gathered),
            len(smalls),
            [*smalls, *sums, *state, target, forward_rows, forward_rows_t, *image_tables],
            [
                partial_shape,
                jax.ShapeDtypeStruct((rows, width), f32),
                jax.ShapeDtypeStruct((2 * rows, cols), f32),
                jax.ShapeDtypeStruct(((count - 2) * rows, cols), f32),
            ],
            source_scratch + image_scratch + adjoint_scratch + band_scratch,
            6 << 30,
            "later_image",
        )
        gathered = True
    sums = exchange(partial, half, jnp.bfloat16)
    args = [half.reshape(1), *sums, *state, forward_cols, forward_rows_t, resist, partner(resist)]
    theta, resist = call(
        functools.partial(last_kernel, count, len(sums)),
        1,
        args,
        [jax.ShapeDtypeStruct((rows, cols), f32)] * 2,
        [pltpu.VMEM((SPLIT * count, 2 * rows, width), f32)] + adjoint_scratch,
        1 << 30,
        "last_step",
    )
    return (theta, resist)


def solution(mesh):
    return jax.shard_map(
        per_device,
        mesh=mesh,
        in_specs=(P(("band", "strip"), None), P(("band", "strip"), None), P("src", None), P("src")),
        out_specs=(P(("band", "strip"), None), P(("band", "strip"), None)),
        check_vma=False,
    )
```

time: 79.2 us -> 57.3 us (0.72)
  Pallas kernels: 28.2 us -> 18.7 us
  blocking collectives: 5.18 us -> 0 us
  starting transfers between devices: 21.9 us -> 16.9 us
  local copies, waits for them, and re-layouts: 5.84 us -> 3.58 us
    ppermute x11 -> x3, starting transfers between devices: 20.2 us -> 3.22 us  [shifted(): lax.ppermute(array, axis, [(i, (i + by) % size) for i in range(size)])]
    ppermute x11 -> x3, waiting for transfers between devices: 15.5 us -> 0.01 us  [shifted(): lax.ppermute(array, axis, [(i, (i + by) % size) for i in range(size)])]
    ppermute x0 -> x7, waiting for transfers between devices: none -> 12.4 us  [fetch(): return lax.ppermute(array, ('strip', 'src'), steps)]
    ppermute x0 -> x7, starting transfers between devices: none -> 10.6 us  [fetch(): return lax.ppermute(array, ('strip', 'src'), steps)]
    pallas_call x3, Pallas kernels: 28.2 us -> 18.7 us  [call(): pl.pallas_call(kernel, out_shape=outs, in_specs=[smem] * n_smem + [vmem]...]
    all_gather x1 -> x0, blocking collectives: 5.18 us -> none  [per_device(): packed = lax.all_gather(packed, 'src', axis=0, tiled=True)]
    ppermute x9 -> x10, waiting for transfers between devices: 0.89 us -> 3.54 us  [partner(): return lax.ppermute(array, 'src', [(i, i ^ 1) for i in range(size)])]
    unnamed x50 -> x22, local copies, waits for them, and re-layouts: 4.22 us -> 2.43 us
  transfers between devices with their start and end apart: 20 -> 20, of which waited for: 6 -> 9; matrix products, arithmetic and copies ran while one was open for 2% -> 2% of each run, Pallas kernels for 0% -> 0%
where the time goes in v2:
time: 57.3 us; the launch traced here: 57.1 us
  Pallas kernels  18.7 us (33%)
  starting transfers between devices  16.9 us (29%)
  waiting for transfers between devices  16 us (28%)
  local copies, waits for them, and re-layouts  3.58 us (6%)
  other arithmetic  1.19 us (2%)
  between operations  0.82 us (1%)
    pallas_call x3, Pallas kernels, call(): pl.pallas_call(kernel, out_shape=outs, in_specs=[smem] * n_smem + [vmem]...  18.7 us
    ppermute x7, waiting for transfers between devices, fetch(): return lax.ppermute(array, ('strip', 'src'), steps)  12.4 us
    ppermute x7, starting transfers between devices, fetch(): return lax.ppermute(array, ('strip', 'src'), steps)  10.6 us
    ppermute x10, waiting for transfers between devices, partner(): return lax.ppermute(array, 'src', [(i, i ^ 1) for i in range(size)])  3.54 us
    ppermute x3, starting transfers between devices, shifted(): lax.ppermute(array, axis, [(i, (i + by) % size) for i in range(size)])  3.22 us
    ppermute x10, starting transfers between devices, partner(): return lax.ppermute(array, 'src', [(i, i ^ 1) for i in range(size)])  3.04 us
    unnamed x22, local copies, waits for them, and re-layouts  2.43 us
  transfers between devices with their start and end apart: 20, of which 9 were waited for; matrix products, arithmetic and copies ran while one was open for 2% of the time, Pallas kernels for 0%

profile of v2, /device:TPU:0, one launch (start us, length us, event | category | flops | bytes accessed | tf_op | source)
XLA Modules:
  0.0 57.1 jit_solution(9016842481291115903)
XLA Ops:
  0.6 0.0 copy-start
  0.7 0.0 copy-start.2
  0.7 1.1 %fusion = (bf16[64,512]{1,0:T(8,128)(2,1)S(1)}, f32[64,512]{1,0:T(8,128)S(1)}) fusion(f32[128,512]{1,0:T(8,128)} %refs_10_.2, pred[]{:T(512)S(6)} %eq.4), kind=kLoop, calls=%fused_computation.8 | loop fusion | flops 65536 | bytes 458753 | tf_op jit(solution)/shard_map/convert_element_type | solution.py:389
  1.7 3.1 %collective-permute-start.3 = (f32[64,512]{1,0:T(8,128)S(1)}, f32[64,512]{1,0:T(8,128)S(1)}, u32[]{:S(2)}, u32[]{:S(2)}) collective-permute-start(f32[64,512]{1,0:T(8,128)S(1)} %get-tuple-element.11), channel_id=1, source_target_pairs={{0,4},{1,13},{2,6},{3,15},{4,8},{5,1},{6,10},{7,3},{8,12},{9,5},{1... | collective-permute-start | bytes 393224 | tf_op jit(solution)/shard_map/ppermute | solution.py:354
  4.9 0.1 copy.13
  4.9 0.1 convert_element_type.16
  5.0 0.1 pad_maximum_fusion.refs_1_
  5.1 2.7 %collective-permute-start.2 = (f32[24]{0:T(128)S(1)}, f32[24]{0:T(128)S(1)}, u32[]{:S(2)}, u32[]{:S(2)}) collective-permute-start(f32[24]{0:T(128)S(1)} %pad_maximum_fusion.refs_1_), channel_id=1, source_target_pairs={{0,3},{1,0},{2,1},{3,2},{4,7},{5,4},{6,5},{7,6},{8,11},{9,8},{10,9... | collective-permute-start | bytes 296 | tf_op jit(solution)/shard_map/ppermute | solution.py:35
  7.8 0.5 collective-permute-start.1
  8.3 0.0 collective-permute-start
  8.3 2.2 %collective-permute-done.3.refs_5_.refs_11_ = f32[64,512]{1,0:T(8,128)S(1)} collective-permute-done((f32[64,512]{1,0:T(8,128)S(1)}, f32[64,512]{1,0:T(8,128)S(1)}, u32[]{:S(2)}, u32[]{:S(2)}) %collective-permute-start.3) | collective-permute-done | bytes 131104 | tf_op jit(solution)/shard_map/ppermute | solution.py:354
  10.5 0.0 collective-permute-start.4
  10.5 1.0 %dynamic-slice_bitcast_fusion.refs_11_.refs_21_ = bf16[256,512]{1,0:T(8,128)(2,1)S(1)} fusion(bf16[2,256,512]{2,1,0:T(8,128)(2,1)} %constant.41.clone, s32[]{:T(128)S(6)} %select_n.46), kind=kLoop, calls=%fused_computation | loop fusion | bytes 524292 | tf_op jit(solution)/shard_map/jit(dynamic_index_in_dim)/squeeze | solution.py:380
  11.5 0.0 copy-start.1
  11.6 0.0 collective-permute-done.2.refs_4_
  11.6 0.0 collective-permute-done.refs_2_
  11.6 0.3 collective-permute-done.4.refs_6_.refs_12_
  11.9 0.6 %copy-done.1 = f32[128,512]{1,0:T(8,128)S(1)} copy-done((f32[128,512]{1,0:T(8,128)S(1)}, f32[128,512]{1,0:T(8,128)}, u32[]{:S(2)}) %copy-start.1) | copy-done | bytes 262168
  12.5 0.9 %copy-done.5 = bf16[256,256]{1,0:T(8,128)(2,1)S(1)} copy-done((bf16[256,256]{1,0:T(8,128)(2,1)S(1)}, bf16[256,256]{1,0:T(8,128)(2,1)}, u32[]{:S(2)}) %copy-start.5) | copy-done | bytes 131096
  13.4 0.9 %copy-done.7 = bf16[256,256]{1,0:T(8,128)(2,1)S(1)} copy-done((bf16[256,256]{1,0:T(8,128)(2,1)S(1)}, bf16[256,256]{1,0:T(8,128)(2,1)}, u32[]{:S(2)}) %copy-start.7) | copy-done | bytes 131096
  14.3 6.7 %first_image.1 = f32[112,256]{1,0:T(8,128)S(1)} custom-call(s32[1]{0:T(128)} %bitcast.refs_0_, f32[24]{0:T(128)S(1)} %pad_maximum_fusion.refs_1_, f32[24]{0:T(128)S(1)} %collective-permute-done.refs_2_, f32[24]{0:T(128)S(1)} %collective-permute-done.1.refs_3_, f32[24]{0:T(128)S(1)} %collective-permute-done.2.refs_4_, ...), custom_call_target="tpu_custom_call" | custom-call | flops 6442450944 | bytes 4194304 | tf_op jit(solution)/shard_map/first_image/pallas_call | solution.py:416
  21.0 0.6 %collective-permute-start.5 = (f32[112,256]{1,0:T(8,128)S(1)}, f32[112,256]{1,0:T(8,128)S(1)}, u32[]{:S(2)}, u32[]{:S(2)}) collective-permute-start(f32[112,256]{1,0:T(8,128)S(1)} %first_image.1), channel_id=1, source_target_pairs={{0,1},{1,0},{2,3},{3,2},{4,5},{5,4},{6,7},{7,6},{8,9},{9,8},{10,11... | collective-permute-start | bytes 344072 | tf_op jit(solution)/shard_map/ppermute | solution.py:40
  21.6 1.8 %collective-permute-start.12 = (bf16[64,512]{1,0:T(8,128)(2,1)S(1)}, bf16[64,512]{1,0:T(8,128)(2,1)S(1)}, u32[]{:S(2)}, u32[]{:S(2)}) collective-permute-start(bf16[64,512]{1,0:T(8,128)(2,1)S(1)} %select_convert_fusion), channel_id=1, source_target_pairs={{0,8},{1,9},{2,10},{3,11},{4,12},{5,13},{6,14},{7,15},{8,0},{9,1},... | collective-permute-start | bytes 196616 | tf_op jit(solution)/shard_map/ppermute | solution.py:354
  23.4 1.1 %collective-permute-start.10 = (bf16[64,512]{1,0:T(8,128)(2,1)S(1)}, bf16[64,512]{1,0:T(8,128)(2,1)S(1)}, u32[]{:S(2)}, u32[]{:S(2)}) collective-permute-start(bf16[64,512]{1,0:T(8,128)(2,1)S(1)} %get-tuple-element.10), channel_id=1, source_target_pairs={{0,12},{1,5},{2,14},{3,7},{4,0},{5,9},{6,2},{7,11},{8,4},{9,13},{1... | collective-permute-start | bytes 196616 | tf_op jit(solution)/shard_map/ppermute | solution.py:354
  24.5 0.0 collective-permute-done.5
  24.5 0.0 copy-start.4
  24.5 1.7 %collective-permute-start.6 = (f32[112,256]{1,0:T(8,128)S(1)}, f32[112,256]{1,0:T(8,128)S(1)}, u32[]{:S(2)}, u32[]{:S(2)}) collective-permute-start(f32[112,256]{1,0:T(8,128)S(1)} %add.20.refs_5_), channel_id=1, source_target_pairs={{0,12},{1,5},{2,14},{3,7},{4,0},{5,9},{6,2},{7,11},{8,4},{9,13},{1... | collective-permute-start | bytes 344072 | tf_op jit(solution)/shard_map/ppermute | solution.py:354
  26.2 0.9 %collective-permute-start.8 = (f32[56,256]{1,0:T(8,128)S(1)}, f32[56,256]{1,0:T(8,128)S(1)}, u32[]{:S(2)}, u32[]{:S(2)}) collective-permute-start(f32[56,256]{1,0:T(8,128)S(1)} %slice_select_fusion.1), channel_id=1, source_target_pairs={{0,8},{1,9},{2,10},{3,11},{4,12},{5,13},{6,14},{7,15},{8,0},{9,1},... | collective-permute-start | bytes 172040 | tf_op jit(solution)/shard_map/ppermute | solution.py:354
  27.0 5.4 %collective-permute-done.6.refs_6_ = f32[112,256]{1,0:T(8,128)S(1)} collective-permute-done((f32[112,256]{1,0:T(8,128)S(1)}, f32[112,256]{1,0:T(8,128)S(1)}, u32[]{:S(2)}, u32[]{:S(2)}) %collective-permute-start.6) | collective-permute-done | bytes 114720 | tf_op jit(solution)/shard_map/ppermute | solution.py:354
  32.5 0.5 collective-permute-start.13
  33.0 0.1 collective-permute-start.11
  33.1 1.3 %collective-permute-done.8.refs_8_ = f32[56,256]{1,0:T(8,128)S(1)} collective-permute-done((f32[56,256]{1,0:T(8,128)S(1)}, f32[56,256]{1,0:T(8,128)S(1)}, u32[]{:S(2)}, u32[]{:S(2)}) %collective-permute-start.8) | collective-permute-done | bytes 57376 | tf_op jit(solution)/shard_map/ppermute | solution.py:354
  34.4 0.0 collective-permute-done.13.refs_16_
  34.4 0.0 collective-permute-done.11.refs_14_
  34.4 1.2 %collective-permute-done.9.refs_9_ = f32[56,256]{1,0:T(8,128)S(1)} collective-permute-done((f32[56,256]{1,0:T(8,128)S(1)}, f32[56,256]{1,0:T(8,128)S(1)}, u32[]{:S(2)}, u32[]{:S(2)}) %collective-permute-start.9) | collective-permute-done | bytes 57376 | tf_op jit(solution)/shard_map/ppermute | solution.py:40
  35.6 0.0 collective-permute-done.7.refs_7_
  35.6 9.0 %later_image.1 = (f32[112,256]{1,0:T(8,128)S(1)}, f32[128,256]{1,0:T(8,128)S(1)}, f32[256,512]{1,0:T(8,128)S(1)}, f32[256,512]{1,0:T(8,128)S(1)}) custom-call(s32[1]{0:T(128)} %bitcast.refs_0_, f32[24]{0:T(128)S(1)} %pad_maximum_fusion.refs_1_, f32[24]{0:T(128)S(1)} %collective-permute-done.refs_2_, f32[24]{0:T(128)S(1)} %collective-permute-done.1.refs_3_, ...), custom_call_target="tpu_custom_call" | custom-call | flops 6442450944 | bytes 4194304 | tf_op jit(solution)/shard_map/later_image/pallas_call | solution.py:416
  44.6 0.2 collective-permute-start.14
  44.9 0.4 collective-permute-start.19
  45.2 0.8 %collective-permute-done.14 = f32[112,256]{1,0:T(8,128)S(1)} collective-permute-done((f32[112,256]{1,0:T(8,128)S(1)}, f32[112,256]{1,0:T(8,128)S(1)}, u32[]{:S(2)}, u32[]{:S(2)}) %collective-permute-start.14) | collective-permute-done | bytes 114720 | tf_op jit(solution)/shard_map/ppermute | solution.py:40
  46.1 2.1 %collective-permute-start.15 = (bf16[112,256]{1,0:T(8,128)(2,1)S(1)}, bf16[112,256]{1,0:T(8,128)(2,1)S(1)}, u32[]{:S(2)}, u32[]{:S(2)}) collective-permute-start(bf16[112,256]{1,0:T(8,128)(2,1)S(1)} %add_convert_fusion.refs_1_), channel_id=1, source_target_pairs={{0,12},{1,5},{2,14},{3,7},{4,0},{5,9},{6,2},{7,11},{8,4},{9,13},{1... | collective-permute-start | bytes 172040 | tf_op jit(solution)/shard_map/ppermute | solution.py:354
  48.2 0.0 collective-permute-start.17
  48.2 2.1 %collective-permute-done.15.refs_2_ = bf16[112,256]{1,0:T(8,128)(2,1)S(1)} collective-permute-done((bf16[112,256]{1,0:T(8,128)(2,1)S(1)}, bf16[112,256]{1,0:T(8,128)(2,1)S(1)}, u32[]{:S(2)}, u32[]{:S(2)}) %collective-permute-start.15) | collective-permute-done | bytes 57376 | tf_op jit(solution)/shard_map/ppermute | solution.py:354
  50.3 1.3 %collective-permute-start.16 = (bf16[112,256]{1,0:T(8,128)(2,1)S(1)}, bf16[112,256]{1,0:T(8,128)(2,1)S(1)}, u32[]{:S(2)}, u32[]{:S(2)}) collective-permute-start(bf16[112,256]{1,0:T(8,128)(2,1)S(1)} %collective-permute-done.15.refs_2_), channel_id=1, source_target_pairs={{0,1},{1,0},{2,3},{3,2},{4,5},{5,4},{6,7},{7,6},{8,9},{9,8},{10,11... | collective-permute-start | bytes 172040 | tf_op jit(solution)/shard_map/ppermute | solution.py:40
  51.6 1.4 %collective-permute-done.17.refs_4_ = bf16[56,256]{1,0:T(8,128)(2,1)S(1)} collective-permute-done((bf16[56,256]{1,0:T(8,128)(2,1)S(1)}, bf16[56,256]{1,0:T(8,128)(2,1)S(1)}, u32[]{:S(2)}, u32[]{:S(2)}) %collective-permute-start.17) | collective-permute-done | bytes 28704 | tf_op jit(solution)/shard_map/ppermute | solution.py:354
  53.0 1.2 %collective-permute-done.18.refs_5_ = bf16[56,256]{1,0:T(8,128)(2,1)S(1)} collective-permute-done((bf16[56,256]{1,0:T(8,128)(2,1)S(1)}, bf16[56,256]{1,0:T(8,128)(2,1)S(1)}, u32[]{:S(2)}, u32[]{:S(2)}) %collective-permute-start.18) | collective-permute-done | bytes 28704 | tf_op jit(solution)/shard_map/ppermute | solution.py:40
  54.2 0.0 collective-permute-done.16.refs_3_
  54.2 3.0 %last_step.1 = (f32[128,512]{1,0:T(8,128)}, f32[128,512]{1,0:T(8,128)}) custom-call(s32[1]{0:T(128)} %bitcast.refs_0_, bf16[112,256]{1,0:T(8,128)(2,1)S(1)} %add_convert_fusion.refs_1_, bf16[112,256]{1,0:T(8,128)(2,1)S(1)} %collective-permute-done.15.refs_2_, bf16[112,256]{1,0:T(8,128)(2,1)S(1)} %collective-permute-done.16.refs_3_, ...), custom_call_target="tpu_custom_call" | custom-call | flops 1073741824 | bytes 4194304 | tf_op jit(solution)/shard_map/last_step/pallas_call | solution.py:416
  (29 shorter events, 0.1 us)
Async XLA Ops:
  0.6 10.9 %copy-start = (s32[128,512]{1,0:T(8,128)S(1)}, s32[128,512]{1,0:T(8,128)}, u32[]{:S(2)}) copy-start(s32[128,512]{1,0:T(8,128)} %param.11) | copy-start | bytes 786436
  0.7 4.2 %copy-start.9 = (s32[8,2]{0,1:T(2,128)S(1)}, s32[8,2]{0,1:T(2,128)}, u32[]{:S(2)}) copy-start(s32[8,2]{0,1:T(2,128)} %param.12) | copy-start | bytes 196
  0.7 4.4 %copy-start.10 = (f32[8]{0:T(128)S(1)}, f32[8]{0:T(128)}, u32[]{:S(2)}) copy-start(f32[8]{0:T(128)} %param.13) | copy-start | bytes 100
  0.7 11.2 %copy-start.2 = (bf16[2,512,256]{2,1,0:T(8,128)(2,1)S(1)}, bf16[2,512,256]{2,1,0:T(8,128)(2,1)}, u32[]{:S(2)}) copy-start(bf16[2,512,256]{2,1,0:T(8,128)(2,1)} %constant.40.clone.refs_10_.refs_20_.refs_8_) | copy-start | bytes 1572868
  1.7 8.8 %collective-permute-start.3 = (f32[64,512]{1,0:T(8,128)S(1)}, f32[64,512]{1,0:T(8,128)S(1)}, u32[]{:S(2)}, u32[]{:S(2)}) collective-permute-start(f32[64,512]{1,0:T(8,128)S(1)} %get-tuple-element.11), channel_id=1, source_target_pairs={{0,4},{1,13},{2,6},{3,15},{4,8},{5,1},{6,10},{7,3},{8,12},{9,5},{1... | collective-permute-start | bytes 393224 | tf_op jit(solution)/shard_map/ppermute | solution.py:354
  5.1 6.5 %collective-permute-start.2 = (f32[24]{0:T(128)S(1)}, f32[24]{0:T(128)S(1)}, u32[]{:S(2)}, u32[]{:S(2)}) collective-permute-start(f32[24]{0:T(128)S(1)} %pad_maximum_fusion.refs_1_), channel_id=1, source_target_pairs={{0,3},{1,0},{2,1},{3,2},{4,7},{5,4},{6,5},{7,6},{8,11},{9,8},{10,9... | collective-permute-start | bytes 296 | tf_op jit(solution)/shard_map/ppermute | solution.py:35
  7.8 3.8 %collective-permute-start.1 = (f32[24]{0:T(128)S(1)}, f32[24]{0:T(128)S(1)}, u32[]{:S(2)}, u32[]{:S(2)}) collective-permute-start(f32[24]{0:T(128)S(1)} %pad_maximum_fusion.refs_1_), channel_id=1, source_target_pairs={{0,2},{1,3},{2,0},{3,1},{4,6},{5,7},{6,4},{7,5},{8,10},{9,11},{10,... | collective-permute-start | bytes 296 | tf_op jit(solution)/shard_map/ppermute | solution.py:35
  8.3 3.3 %collective-permute-start = (f32[24]{0:T(128)S(1)}, f32[24]{0:T(128)S(1)}, u32[]{:S(2)}, u32[]{:S(2)}) collective-permute-start(f32[24]{0:T(128)S(1)} %pad_maximum_fusion.refs_1_), channel_id=1, source_target_pairs={{0,1},{1,2},{2,3},{3,0},{4,5},{5,6},{6,7},{7,4},{8,9},{9,10},{10,1... | collective-permute-start | bytes 296 | tf_op jit(solution)/shard_map/ppermute | solution.py:35
  8.3 3.6 %copy-start.3 = (bf16[3,256,160]{2,1,0:T(8,128)(2,1)S(1)}, bf16[3,256,160]{2,1,0:T(8,128)(2,1)}, u32[]{:S(2)}) copy-start(bf16[3,256,160]{2,1,0:T(8,128)(2,1)} %constant.42.clone.refs_12_.refs_22_) | copy-start | bytes 737284
  10.5 1.3 %collective-permute-start.4 = (f32[64,512]{1,0:T(8,128)S(1)}, f32[64,512]{1,0:T(8,128)S(1)}, u32[]{:S(2)}, u32[]{:S(2)}) collective-permute-start(f32[64,512]{1,0:T(8,128)S(1)} %collective-permute-done.3.refs_5_.refs_11_), channel_id=1, source_target_pairs={{0,1},{1,0},{2,3},{3,2},{4,5},{5,4},{6,7},{7,6},{8,9},{9,8},{10,11... | collective-permute-start | bytes 393224 | tf_op jit(solution)/shard_map/ppermute | solution.py:40
  11.5 1.0 %copy-start.1 = (f32[128,512]{1,0:T(8,128)S(1)}, f32[128,512]{1,0:T(8,128)}, u32[]{:S(2)}) copy-start(f32[128,512]{1,0:T(8,128)} %refs_10_.2) | copy-start | bytes 786436
  12.5 0.9 %copy-start.5 = (bf16[256,256]{1,0:T(8,128)(2,1)S(1)}, bf16[256,256]{1,0:T(8,128)(2,1)}, u32[]{:S(2)}) copy-start(bf16[256,256]{1,0:T(8,128)(2,1)} %constant.43.clone.refs_13_.refs_23_) | copy-start | bytes 393220
  13.4 0.9 %copy-start.7 = (bf16[256,256]{1,0:T(8,128)(2,1)S(1)}, bf16[256,256]{1,0:T(8,128)(2,1)}, u32[]{:S(2)}) copy-start(bf16[256,256]{1,0:T(8,128)(2,1)} %constant.38.clone.refs_9_.refs_18_) | copy-start | bytes 393220
  21.0 3.4 %collective-permute-start.5 = (f32[112,256]{1,0:T(8,128)S(1)}, f32[112,256]{1,0:T(8,128)S(1)}, u32[]{:S(2)}, u32[]{:S(2)}) collective-permute-start(f32[112,256]{1,0:T(8,128)S(1)} %first_image.1), channel_id=1, source_target_pairs={{0,1},{1,0},{2,3},{3,2},{4,5},{5,4},{6,7},{7,6},{8,9},{9,8},{10,11... | collective-permute-start | bytes 344072 | tf_op jit(solution)/shard_map/ppermute | solution.py:40
  21.6 10.9 %collective-permute-start.12 = (bf16[64,512]{1,0:T(8,128)(2,1)S(1)}, bf16[64,512]{1,0:T(8,128)(2,1)S(1)}, u32[]{:S(2)}, u32[]{:S(2)}) collective-permute-start(bf16[64,512]{1,0:T(8,128)(2,1)S(1)} %select_convert_fusion), channel_id=1, source_target_pairs={{0,8},{1,9},{2,10},{3,11},{4,12},{5,13},{6,14},{7,15},{8,0},{9,1},... | collective-permute-start | bytes 196616 | tf_op jit(solution)/shard_map/ppermute | solution.py:354
  23.4 9.6 %collective-permute-start.10 = (bf16[64,512]{1,0:T(8,128)(2,1)S(1)}, bf16[64,512]{1,0:T(8,128)(2,1)S(1)}, u32[]{:S(2)}, u32[]{:S(2)}) collective-permute-start(bf16[64,512]{1,0:T(8,128)(2,1)S(1)} %get-tuple-element.10), channel_id=1, source_target_pairs={{0,12},{1,5},{2,14},{3,7},{4,0},{5,9},{6,2},{7,11},{8,4},{9,13},{1... | collective-permute-start | bytes 196616 | tf_op jit(solution)/shard_map/ppermute | solution.py:354
  24.5 11.2 %copy-start.6 = (bf16[256,256]{1,0:T(8,128)(2,1)S(1)}, bf16[256,256]{1,0:T(8,128)(2,1)}, u32[]{:S(2)}) copy-start(bf16[256,256]{1,0:T(8,128)(2,1)} %constant.43.clone.refs_13_.refs_23_) | copy-start | bytes 393220
  24.5 11.2 %copy-start.8 = (bf16[256,256]{1,0:T(8,128)(2,1)S(1)}, bf16[256,256]{1,0:T(8,128)(2,1)}, u32[]{:S(2)}) copy-start(bf16[256,256]{1,0:T(8,128)(2,1)} %constant.38.clone.refs_9_.refs_18_) | copy-start | bytes 393220
  24.5 11.1 %copy-start.4 = (bf16[256,256]{1,0:T(8,128)(2,1)S(1)}, bf16[256,256]{1,0:T(8,128)(2,1)}, u32[]{:S(2)}) copy-start(bf16[256,256]{1,0:T(8,128)(2,1)} %constant.39.clone.refs_19_.refs_9_) | copy-start | bytes 393220
  24.5 8.0 %collective-permute-start.6 = (f32[112,256]{1,0:T(8,128)S(1)}, f32[112,256]{1,0:T(8,128)S(1)}, u32[]{:S(2)}, u32[]{:S(2)}) collective-permute-start(f32[112,256]{1,0:T(8,128)S(1)} %add.20.refs_5_), channel_id=1, source_target_pairs={{0,12},{1,5},{2,14},{3,7},{4,0},{5,9},{6,2},{7,11},{8,4},{9,13},{1... | collective-permute-start | bytes 344072 | tf_op jit(solution)/shard_map/ppermute | solution.py:354
  26.2 8.2 %collective-permute-start.8 = (f32[56,256]{1,0:T(8,128)S(1)}, f32[56,256]{1,0:T(8,128)S(1)}, u32[]{:S(2)}, u32[]{:S(2)}) collective-permute-start(f32[56,256]{1,0:T(8,128)S(1)} %slice_select_fusion.1), channel_id=1, source_target_pairs={{0,8},{1,9},{2,10},{3,11},{4,12},{5,13},{6,14},{7,15},{8,0},{9,1},... | collective-permute-start | bytes 172040 | tf_op jit(solution)/shard_map/ppermute | solution.py:354
  32.5 3.1 %collective-permute-start.7 = (f32[112,256]{1,0:T(8,128)S(1)}, f32[112,256]{1,0:T(8,128)S(1)}, u32[]{:S(2)}, u32[]{:S(2)}) collective-permute-start(f32[112,256]{1,0:T(8,128)S(1)} %collective-permute-done.6.refs_6_), channel_id=1, source_target_pairs={{0,1},{1,0},{2,3},{3,2},{4,5},{5,4},{6,7},{7,6},{8,9},{9,8},{10,11... | collective-permute-start | bytes 344072 | tf_op jit(solution)/shard_map/ppermute | solution.py:40
  32.5 1.9 %collective-permute-start.13 = (bf16[64,512]{1,0:T(8,128)(2,1)S(1)}, bf16[64,512]{1,0:T(8,128)(2,1)S(1)}, u32[]{:S(2)}, u32[]{:S(2)}) collective-permute-start(bf16[64,512]{1,0:T(8,128)(2,1)S(1)} %collective-permute-done.12.refs_15_), channel_id=1, source_target_pairs={{0,1},{1,0},{2,3},{3,2},{4,5},{5,4},{6,7},{7,6},{8,9},{9,8},{10,11... | collective-permute-start | bytes 196616 | tf_op jit(solution)/shard_map/ppermute | solution.py:40
  33.0 1.4 %collective-permute-start.11 = (bf16[64,512]{1,0:T(8,128)(2,1)S(1)}, bf16[64,512]{1,0:T(8,128)(2,1)S(1)}, u32[]{:S(2)}, u32[]{:S(2)}) collective-permute-start(bf16[64,512]{1,0:T(8,128)(2,1)S(1)} %collective-permute-done.10.refs_13_), channel_id=1, source_target_pairs={{0,1},{1,0},{2,3},{3,2},{4,5},{5,4},{6,7},{7,6},{8,9},{9,8},{10,11... | collective-permute-start | bytes 196616 | tf_op jit(solution)/shard_map/ppermute | solution.py:40
  34.4 1.2 %collective-permute-start.9 = (f32[56,256]{1,0:T(8,128)S(1)}, f32[56,256]{1,0:T(8,128)S(1)}, u32[]{:S(2)}, u32[]{:S(2)}) collective-permute-start(f32[56,256]{1,0:T(8,128)S(1)} %collective-permute-done.8.refs_8_), channel_id=1, source_target_pairs={{0,1},{1,0},{2,3},{3,2},{4,5},{5,4},{6,7},{7,6},{8,9},{9,8},{10,11... | collective-permute-start | bytes 172040 | tf_op jit(solution)/shard_map/ppermute | solution.py:40
  44.6 1.4 %collective-permute-start.14 = (f32[112,256]{1,0:T(8,128)S(1)}, f32[112,256]{1,0:T(8,128)S(1)}, u32[]{:S(2)}, u32[]{:S(2)}) collective-permute-start(f32[112,256]{1,0:T(8,128)S(1)} %get-tuple-element.6), channel_id=1, source_target_pairs={{0,1},{1,0},{2,3},{3,2},{4,5},{5,4},{6,7},{7,6},{8,9},{9,8},{10,11... | collective-permute-start | bytes 344072 | tf_op jit(solution)/shard_map/ppermute | solution.py:40
  44.9 8.1 %collective-permute-start.19 = (f32[128,256]{1,0:T(8,128)S(1)}, f32[128,256]{1,0:T(8,128)S(1)}, u32[]{:S(2)}, u32[]{:S(2)}) collective-permute-start(f32[128,256]{1,0:T(8,128)S(1)} %get-tuple-element.9.refs_10_), channel_id=1, source_target_pairs={{0,1},{1,0},{2,3},{3,2},{4,5},{5,4},{6,7},{7,6},{8,9},{9,8},{10,11... | collective-permute-start | bytes 393224 | tf_op jit(solution)/shard_map/ppermute | solution.py:40
  46.1 4.2 %collective-permute-start.15 = (bf16[112,256]{1,0:T(8,128)(2,1)S(1)}, bf16[112,256]{1,0:T(8,128)(2,1)S(1)}, u32[]{:S(2)}, u32[]{:S(2)}) collective-permute-start(bf16[112,256]{1,0:T(8,128)(2,1)S(1)} %add_convert_fusion.refs_1_), channel_id=1, source_target_pairs={{0,12},{1,5},{2,14},{3,7},{4,0},{5,9},{6,2},{7,11},{8,4},{9,13},{1... | collective-permute-start | bytes 172040 | tf_op jit(solution)/shard_map/ppermute | solution.py:354
  48.2 4.8 %collective-permute-start.17 = (bf16[56,256]{1,0:T(8,128)(2,1)S(1)}, bf16[56,256]{1,0:T(8,128)(2,1)S(1)}, u32[]{:S(2)}, u32[]{:S(2)}) collective-permute-start(bf16[56,256]{1,0:T(8,128)(2,1)S(1)} %slice_select_fusion.2), channel_id=1, source_target_pairs={{0,8},{1,9},{2,10},{3,11},{4,12},{5,13},{6,14},{7,15},{8,0},{9,1},... | collective-permute-start | bytes 86024 | tf_op jit(solution)/shard_map/ppermute | solution.py:354
  50.3 3.9 %collective-permute-start.16 = (bf16[112,256]{1,0:T(8,128)(2,1)S(1)}, bf16[112,256]{1,0:T(8,128)(2,1)S(1)}, u32[]{:S(2)}, u32[]{:S(2)}) collective-permute-start(bf16[112,256]{1,0:T(8,128)(2,1)S(1)} %collective-permute-done.15.refs_2_), channel_id=1, source_target_pairs={{0,1},{1,0},{2,3},{3,2},{4,5},{5,4},{6,7},{7,6},{8,9},{9,8},{10,11... | collective-permute-start | bytes 172040 | tf_op jit(solution)/shard_map/ppermute | solution.py:40
  53.0 1.2 %collective-permute-start.18 = (bf16[56,256]{1,0:T(8,128)(2,1)S(1)}, bf16[56,256]{1,0:T(8,128)(2,1)S(1)}, u32[]{:S(2)}, u32[]{:S(2)}) collective-permute-start(bf16[56,256]{1,0:T(8,128)(2,1)S(1)} %collective-permute-done.17.refs_4_), channel_id=1, source_target_pairs={{0,1},{1,0},{2,3},{3,2},{4,5},{5,4},{6,7},{7,6},{8,9},{9,8},{10,11... | collective-permute-start | bytes 86024 | tf_op jit(solution)/shard_map/ppermute | solution.py:40
